TPU v7x, 128 devices: a whole 4x4x4 slice. The times are simulated.
128 devices in a mesh: az: 8 (over y, core), rg: 16 (over z, x).
Axes of the slice: x: 4, y: 4, z: 4, core: 2. Of those that a mesh axis runs over, the one named last changes fastest.
Arguments:
- master_raw: float32 [2, 2048, 20000], P(None, 'az', 'rg'), may hold values from -6 to 6
- slave_raw: float32 [2, 2048, 20000], P(None, 'az', 'rg'), may hold values from -6 to 6
- range_ref: float32 [2, 20000], replicated, may hold values from -4 to 4
- az_ref: float32 [2, 2048], replicated, may hold values from -4 to 4
- az_shift: int32 [4, 256], P(None, ('az', 'rg')), may hold values from -32 to 32, as said below
- rg_shift: int32 [4, 256], P(None, ('az', 'rg')), may hold values from -64 to 64, as said below
- valid_lines: int32 [256], replicated, may hold values from 1024 to 2048, as said below
Outputs:
- interferogram: float32 [2, 256, 2048], P(None, None, ('az', 'rg'))
Inputs may be any that keep to these rules, and one draw needn't show every extreme that they name: `az_shift`: azimuth offset of the slave in lines for each block of 512 lines and 64 samples. `rg_shift`: range offset of the slave in samples for each block of 512 lines and 64 samples. Lines 0 to valid_lines[t] - 1 of range tile t are valid.
All inputs are finite; a program needn't handle non-finite values.
Results may differ from a plain program's by a relative error of at most 0.0003.
Values sent between devices are 32-bit elements; how exact they have to be, the bound alone decides.
No kernel may reach another device: no remote copies, remote signals or barrier semaphores. Data moves between devices by JAX's collectives and lax.ppermute only.
A program may use at most 256 MiB of HBM per device.

v0:
```python
import math

import jax
import jax.numpy as jnp
import numpy as np
from jax import lax
from jax.experimental import pallas as pl
from jax.experimental.pallas import tpu as pltpu
from jax.sharding import PartitionSpec as P


LINES = 2048
RANGE = 20000
LOOK = 8
BA = 512
BR = 64
ASH = 32
RSH = 64
NBA = 4
ALL = ("az", "rg")
NP = 16
NQ = 10
NS = 125
F32 = jnp.float32
BF16 = jnp.bfloat16


SHIFTS = sorted(
    ((dx, dz) for dx in range(4) for dz in range(4)),
    key=lambda s: -(min(s[0], 4 - s[0]) + min(s[1], 4 - s[1])),
)


def shifted(r, shift):
    return ((r // 4 + shift[1]) % 4) * 4 + (r % 4 + shift[0]) % 4


def _rot(v, angle):
    c, s = math.cos(angle), math.sin(angle)
    turns = angle / (math.pi / 4)
    eighth = round(turns)
    x, y = v
    if abs(turns - eighth) < 1e-9:
        e = eighth % 8
        if e == 0:
            return v
        if e == 2:
            return (-y, x)
        if e == 4:
            return (-x, -y)
        if e == 6:
            return (y, -x)
        h = math.sqrt(0.5)
        if e == 1:
            return ((x - y) * h, (x + y) * h)
        if e == 3:
            return (-(x + y) * h, (x - y) * h)
        if e == 5:
            return ((y - x) * h, -(x + y) * h)
        return ((x + y) * h, (y - x) * h)
    return (x * c - y * s, x * s + y * c)


def _add(a, b):
    return (a[0] + b[0], a[1] + b[1])


def _sub(a, b):
    return (a[0] - b[0], a[1] - b[1])


def _dft2(v, sign):
    return [_add(v[0], v[1]), _sub(v[0], v[1])]


def _dft4(v, sign):
    a, b = _add(v[0], v[2]), _sub(v[0], v[2])
    c, d = _add(v[1], v[3]), _sub(v[1], v[3])
    if sign < 0:
        return [_add(a, c), (b[0] + d[1], b[1] - d[0]), _sub(a, c), (b[0] - d[1], b[1] + d[0])]
    return [_add(a, c), (b[0] - d[1], b[1] + d[0]), _sub(a, c), (b[0] + d[1], b[1] - d[0])]


def _dft5(v, sign):
    c1, c2 = math.cos(2 * math.pi / 5), math.cos(4 * math.pi / 5)
    s1, s2 = sign * math.sin(2 * math.pi / 5), sign * math.sin(4 * math.pi / 5)
    a1, b1 = _add(v[1], v[4]), _sub(v[1], v[4])
    a2, b2 = _add(v[2], v[3]), _sub(v[2], v[3])
    x0 = v[0]
    y0 = (x0[0] + a1[0] + a2[0], x0[1] + a1[1] + a2[1])
    p1 = tuple(x0[i] + c1 * a1[i] + c2 * a2[i] for i in range(2))
    p2 = tuple(x0[i] + c2 * a1[i] + c1 * a2[i] for i in range(2))
    q1 = tuple(s1 * b1[i] + s2 * b2[i] for i in range(2))
    q2 = tuple(s2 * b1[i] - s1 * b2[i] for i in range(2))
    return [
        y0,
        (p1[0] - q1[1], p1[1] + q1[0]),
        (p2[0] - q2[1], p2[1] + q2[0]),
        (p2[0] + q2[1], p2[1] - q2[0]),
        (p1[0] + q1[1], p1[1] - q1[0]),
    ]


def _dft_two(v, n1, n2, first, second, sign):
    n = n1 * n2
    out = [None] * n
    mid = []
    for b in range(n2):
        col = first([v[n2 * a + b] for a in range(n1)], sign)
        mid.append([_rot(col[k], sign * 2 * math.pi * ((b * k) % n) / n) for k in range(n1)])
    for k1 in range(n1):
        row = second([mid[b][k1] for b in range(n2)], sign)
        for k2 in range(n2):
            out[k1 + n1 * k2] = row[k2]
    return out


def dft16(v, sign):
    return _dft_two(v, 4, 4, _dft4, _dft4, sign)


def dft10(v, sign):
    return _dft_two(v, 2, 5, _dft2, _dft5, sign)


def cmul(a, b):
    return (a[0] * b[0] - a[1] * b[1], a[0] * b[1] + a[1] * b[0])


def split(x):
    hi = x.astype(BF16)
    return hi, (x - hi.astype(F32)).astype(BF16)


def dot(a, b):
    return jnp.dot(a, b, preferred_element_type=F32)


def worker(block):
    y, rest = divmod(block, 32)
    c, rest = divmod(rest, 16)
    z, x = divmod(rest, 4)
    pair, core = divmod(x, 2)
    return (y * 2 + core) * 16 + z * 4 + 2 * c + (pair + z) % 2


def block_of(az, rg):
    y, core = az // 2, az % 2
    z, x = rg // 4, rg % 4
    return y * 32 + (x // 2) * 16 + z * 4 + 2 * ((x + z) % 2) + core


def _np_split(x):
    x = np.asarray(x, np.float32)
    hi = x.astype(BF16)
    return hi, (x - hi.astype(np.float32)).astype(BF16)


def _tables():
    t = {}
    two = 2 * np.pi
    q2 = np.arange(128)
    keep = (q2 < NS)[None, :]
    ang = -two * ((np.arange(NQ)[:, None] * q2[None, :]) % 1250) / 1250
    t["twb"] = np.stack([np.cos(ang) * keep, np.sin(ang) * keep], 1).astype(np.float32)
    n = np.arange(NQ)[None, :, None] * NS + q2[None, None, :]
    ang = two * ((np.arange(NP)[:, None, None] * n) % RANGE) / RANGE
    t["twc"] = np.stack([np.cos(ang), np.sin(ang)], 2).reshape(NP * NQ, 2, 128).astype(np.float32)
    ang = two * ((q2[:, None] * q2[None, :]) % NS) / NS
    both = keep & keep.T
    c, s = np.cos(ang) * both, np.sin(ang) * both
    t["fh"], t["fl"] = _np_split(np.block([[c, -s], [s, c]]))
    t["gh"], t["gl"] = _np_split(np.block([[c, s], [-s, c]]))
    k2 = np.arange(128)
    back = (-np.arange(128)) % 128
    ang = two * ((k2[:, None] * back[None, :]) % 128) / 128
    t["dft"] = np.stack([np.cos(ang), np.sin(ang)]).astype(np.float32)
    ang = two * (np.arange(16)[:, None] * back[None, :]) / LINES
    t["turn"] = np.stack([np.cos(ang), np.sin(ang)]).astype(np.float32)
    ang = np.broadcast_to(-two * np.arange(16)[:, None] / 16, (16, 128))
    t["wrap"] = np.stack([np.cos(ang), np.sin(ang)], 1).astype(np.float32)
    lane = np.arange(128)
    pick = np.zeros((24, 128), np.float32)
    for o in range(16):
        pick[o] = np.abs(lane // LOOK - o) <= 1
    pick[16] = lane < LOOK
    pick[17] = lane >= 128 - LOOK
    t["pick"] = pick
    return t


TABLES = _tables()


HBM = pl.BlockSpec(memory_space=pltpu.HBM)
VMEM = pl.BlockSpec(memory_space=pltpu.VMEM)
SMEM = pl.BlockSpec(memory_space=pltpu.SMEM)


AZIMUTH_MIB = 61
MASTER_MIB = 61


def limit(mib):
    return pltpu.CompilerParams(vmem_limit_bytes=mib << 20)


def _raw_rows(raw):
    raw = raw.transpose(2, 0, 1).reshape(1250, 2, 2, 128)
    return raw.transpose(0, 2, 1, 3).reshape(5000, 128)


def _read_lines(x_hbm, x_ref, t_ref, sem, done):
    def load(q):
        rows = pl.ds(1000 * q, 1000)
        return pltpu.make_async_copy(x_hbm.at[rows], x_ref.at[rows], sem.at[q])

    for q in range(5):
        load(q).start()
    for q in range(NQ):
        if q % 2 == 0:
            load(q // 2).wait()
        for half in range(2):
            for c in range(2):
                v = x_ref[pl.ds(500 * q + 2 * half + c, NS, stride=4), :]
                v = jnp.concatenate([v, jnp.zeros((128 - NS, 128), F32)], axis=0).T
                for k in range(8):
                    t_ref[8 * half + k, q, c] = v[16 * k : 16 * k + 16]
        done(q)


def _pre_kernel(x_hbm, o_hbm, x_ref, t_ref, sem):
    def store(q):
        at = pl.ds(2 * (q // 2), 2)
        return pltpu.make_async_copy(t_ref.at[:, at], o_hbm.at[:, at], sem.at[5 + q // 2])

    _read_lines(x_hbm, x_ref, t_ref, sem, lambda q: store(q).start() if q % 2 else None)
    for q in range(0, NQ, 2):
        store(q).wait()


def _pre_shift_kernel(me_ref, x_hbm, *refs):
    outs, (x_ref, t_ref, sem) = refs[:NP], refs[NP:]
    _read_lines(x_hbm, x_ref, t_ref, sem, lambda q: None)
    me = me_ref[0]
    stores = [
        pltpu.make_async_copy(t_ref.at[shifted(me, shift)], o_hbm, sem.at[5 + k])
        for k, (shift, o_hbm) in enumerate(zip(SHIFTS, outs))
    ]
    for store in stores:
        store.start()
    for store in stores:
        store.wait()


PRE_SCRATCH = [
    pltpu.VMEM((5000, 128), F32),
    pltpu.VMEM((NP, NQ, 2, 16, 128), F32),
    pltpu.SemaphoreType.DMA((5 + NP,)),
]


def pre(raw):
    return pl.pallas_call(
        _pre_kernel,
        in_specs=[HBM],
        out_specs=HBM,
        out_shape=jax.ShapeDtypeStruct((NP, NQ, 2, 16, 128), F32),
        scratch_shapes=PRE_SCRATCH,
        cost_estimate=pl.CostEstimate(flops=10**8, bytes_accessed=10**7, transcendentals=0),
        name="pre",
    )(_raw_rows(raw))


def pre_shifts(me, raw):
    return pl.pallas_call(
        _pre_shift_kernel,
        in_specs=[SMEM, HBM],
        out_specs=[HBM] * NP,
        out_shape=[jax.ShapeDtypeStruct((NQ, 2, 16, 128), F32)] * NP,
        scratch_shapes=PRE_SCRATCH,
        cost_estimate=pl.CostEstimate(flops=10**8, bytes_accessed=10**7, transcendentals=0),
        name="pre_shifts",
    )(me, _raw_rows(raw))


def _range_body(ready, tables, o_hbm, d_ref, x_ref, o_ref, out_sem):
    twb_ref, hf_ref, fh_ref, fl_ref, gh_ref, gl_ref, twc_ref = tables
    lane = lax.broadcasted_iota(jnp.int32, (16, 128), 1)

    def outer(q, carry):
        ready(q)
        for g in range(2):
            rows = slice(8 * g, 8 * g + 8)
            v = [(x_ref[p, q, 0, rows, :], x_ref[p, q, 1, rows, :]) for p in range(NP)]
            v = dft16(v, -1)
            for k in range(NP):
                at = k * NQ + q
                r, i = cmul(v[k], (twc_ref[at, 0:1, :], -twc_ref[at, 1:2, :]))
                d_ref[at, 0, rows, :] = r
                d_ref[at, 1, rows, :] = i
        return carry

    lax.fori_loop(0, NQ, outer, 0, unroll=2)
    ready(None)

    def middle(kp, carry):
        v = [(d_ref[kp * NQ + q, 0], d_ref[kp * NQ + q, 1]) for q in range(NQ)]
        v = dft10(v, -1)
        rows = []
        for k in range(NQ):
            r, i = cmul(v[k], (twb_ref[k, 0:1, :], twb_ref[k, 1:2, :]))
            rows.append(jnp.concatenate([r, i], axis=1))
        hi, lo = split(jnp.concatenate(rows, axis=0))
        y = dot(hi, fh_ref[...]) + dot(lo, fh_ref[...]) + dot(hi, fl_ref[...])
        rows = []
        for k in range(NQ):
            val = (y[16 * k : 16 * k + 16, :128], y[16 * k : 16 * k + 16, 128:])
            r, i = cmul(val, (hf_ref[kp * NQ + k, 0:1, :], hf_ref[kp * NQ + k, 1:2, :]))
            rows.append(jnp.concatenate([r, i], axis=1))
        hi, lo = split(jnp.concatenate(rows, axis=0))
        y = dot(hi, gh_ref[...]) + dot(lo, gh_ref[...]) + dot(hi, gl_ref[...])
        v = []
        for k in range(NQ):
            val = (y[16 * k : 16 * k + 16, :128], y[16 * k : 16 * k + 16, 128:])
            v.append(cmul(val, (twb_ref[k, 0:1, :], -twb_ref[k, 1:2, :])))
        v = dft10(v, 1)
        for q in range(NQ):
            at = kp * NQ + q
            r, i = cmul(v[q], (twc_ref[at, 0:1, :], twc_ref[at, 1:2, :]))
            d_ref[at, 0] = r
            d_ref[at, 1] = i
        return carry

    lax.fori_loop(0, NP, middle, 0, unroll=4)

    def inner(q, carry):
        for g in range(2):
            rows = slice(8 * g, 8 * g + 8)
            v = [(d_ref[k * NQ + q, 0, rows, :], d_ref[k * NQ + q, 1, rows, :]) for k in range(NP)]
            v = dft16(v, 1)
            for p in range(14):
                d_ref[p * NQ + q, 0, rows, :] = v[p][0]
                d_ref[p * NQ + q, 1, rows, :] = v[p][1]
        return carry

    lax.fori_loop(0, NQ, inner, 0, unroll=2)

    def store(part):
        at = pl.ds(32 * part, 32)
        return pltpu.make_async_copy(o_ref.at[at], o_hbm.at[at], out_sem.at[part])

    for d in range(128):
        n, a = divmod(128 * d, NS)
        for c in range(2):
            val = d_ref[n, c]
            if a:
                val = pltpu.roll(val, 128 - a, 1)
            start = NS - a
            while start < 128:
                n2 = (128 * d + start) // NS
                nxt = d_ref[n2, c]
                nxt = pltpu.roll(nxt, start % 128, 1)
                val = jnp.where(lane < start, val, nxt)
                start += NS
            o_ref[worker(d), c] = val
        if d % 32 == 31:
            store(d // 32).start()
    for part in range(4):
        store(part).wait()


def _tables_in(table_hbm, tables, sem):
    copies = [
        pltpu.make_async_copy(src, dst, sem.at[k]) for k, (src, dst) in enumerate(zip(table_hbm, tables))
    ]
    for copy in copies[::-1]:
        copy.start()
    return copies


def _range_kernel(x_hbm, *refs):
    table_hbm, o_hbm, tables, (d_ref, x_ref, o_ref, out_sem, in_sem, sem) = refs[:7], refs[7], refs[8:15], refs[15:]

    def load(q):
        return pltpu.make_async_copy(x_hbm.at[:, q], x_ref.at[:, q], in_sem.at[q])

    def ready(q):
        if q is None:
            for copy in copies[:6]:
                copy.wait()
        else:
            load(q).wait()

    copies = _tables_in(table_hbm, tables, sem)
    for q in range(NQ):
        load(q).start()
    copies[6].wait()
    _range_body(ready, tables, o_hbm, d_ref, x_ref, o_ref, out_sem)


def _range_shift_kernel(me_ref, *refs):
    parts, refs = refs[:NP], refs[NP:]
    table_hbm, o_hbm, tables, (d_ref, x_ref, o_ref, out_sem, in_sem, sem) = refs[:7], refs[7], refs[8:15], refs[15:]
    me = me_ref[0]
    loads = [
        pltpu.make_async_copy(
            part, x_ref.at[shifted(me, (4 - shift[0], 4 - shift[1]))], in_sem.at[k]
        )
        for k, (shift, part) in enumerate(zip(SHIFTS, parts))
    ]

    def ready(q):
        if q is None:
            for copy in copies[:6]:
                copy.wait()

    copies = _tables_in(table_hbm, tables, sem)
    for load in loads:
        load.start()
    for load in loads:
        load.wait()
    copies[6].wait()
    _range_body(ready, tables, o_hbm, d_ref, x_ref, o_ref, out_sem)


def range_compress(kernel, specs, operands, hf):
    t = TABLES
    tables = (t["twb"], hf, t["fh"], t["fl"], t["gh"], t["gl"], t["twc"])
    return pl.pallas_call(
        kernel,
        in_specs=specs + [HBM] * 7,
        out_specs=HBM,
        out_shape=jax.ShapeDtypeStruct((128, 2, 16, 128), F32),
        scratch_shapes=[pltpu.VMEM(x.shape, x.dtype) for x in tables]
        + [
            pltpu.VMEM((NP * NQ, 2, 16, 128), F32),
            pltpu.VMEM((NP, NQ, 2, 16, 128), F32),
            pltpu.VMEM((128, 2, 16, 128), F32),
            pltpu.SemaphoreType.DMA((4,)),
            pltpu.SemaphoreType.DMA((NP,)),
            pltpu.SemaphoreType.DMA((7,)),
        ],
        cost_estimate=pl.CostEstimate(flops=10**10, bytes_accessed=6 * 10**6, transcendentals=0),
    )(*operands, *tables)


def _dot_t(a, b):
    return lax.dot_general(
        a, b, (((1,), (1,)), ((), ())), precision=lax.Precision.HIGHEST, preferred_element_type=F32
    )


def _prep_kernel(h_ref, dft_ref, turn_ref, wrap_ref, a_ref, g_ref):
    def mul(a, b):
        return jnp.dot(a, b, precision=lax.Precision.HIGHEST, preferred_element_type=F32)

    hr, hi = h_ref[0], h_ref[1]
    dr, di = dft_ref[0], dft_ref[1]
    g = (mul(hr, dr) - mul(hi, di), mul(hr, di) + mul(hi, dr))
    r, i = cmul(g, (turn_ref[0], turn_ref[1]))
    g_ref[:, 0, :] = r
    g_ref[:, 1, :] = i
    row = lax.broadcasted_iota(jnp.int32, (128, 128), 0)
    lane = lax.broadcasted_iota(jnp.int32, (128, 128), 1)
    over = lane > row

    def body(k, carry):
        m = []
        for c in range(2):
            line = jnp.broadcast_to(g_ref[k, c : c + 1, :], (128, 128))
            m.append(pltpu.roll(line, 0, 1, stride=1, stride_axis=0))
        turned = cmul(m, (wrap_ref[k, 0:1, :], wrap_ref[k, 1:2, :]))
        re = jnp.where(over, turned[0], m[0])
        im = jnp.where(over, turned[1], m[1])
        for part, block in enumerate((re, -im)):
            cols = slice(128 * part, 128 * part + 128)
            high, low = split(block)
            a_ref[k, 0:128, cols] = high
            a_ref[k, 128:256, cols] = low
        return carry

    lax.fori_loop(0, 16, body, 0, unroll=2)


def prep(h):
    t = TABLES
    return pl.pallas_call(
        _prep_kernel,
        out_shape=jax.ShapeDtypeStruct((16, 256, 256), BF16),
        scratch_shapes=[pltpu.VMEM((16, 2, 128), F32)],
        cost_estimate=pl.CostEstimate(flops=2 * 10**9, bytes_accessed=5 * 10**6, transcendentals=0),
        name="prep",
    )(h, t["dft"], t["turn"], t["wrap"])


def _azimuth_front(x_hbm, a_hbm, e_ref, x_ref, a_ref, sem):
    def load(s):
        return pltpu.make_async_copy(x_hbm.at[:, s], x_ref.at[:, s], sem.at[s])

    matrices = pltpu.make_async_copy(a_hbm, a_ref, sem.at[8])
    for s in range(8):
        load(s).start()
    matrices.start()

    def first(s, carry):
        load(s).wait()
        for g in range(2):
            rows = slice(8 * g, 8 * g + 8)
            v = [(x_ref[a, s, 0, rows, :], x_ref[a, s, 1, rows, :]) for a in range(16)]
            v = dft16(v, -1)
            for k in range(16):
                for c in range(2):
                    at = pl.multiple_of(c * 128 + s * 16 + g * 8, 8)
                    e_ref[k, pl.ds(at, 8), :] = v[k][c]
        return carry

    lax.fori_loop(0, 8, first, 0, unroll=2)
    matrices.wait()

    def second(k, carry):
        re_hi, re_lo = split(e_ref[k, 0:128, :])
        im_hi, im_lo = split(e_ref[k, 128:256, :])

        def turned(re, im):
            straight = jnp.concatenate([re, im], axis=0)
            return jnp.concatenate([straight, jnp.concatenate([im, -re], axis=0)], axis=1)

        y = dot(a_ref[k], turned(re_hi, im_hi))
        y = y[:128] + y[128:] + dot(a_ref[k, 0:128, :], turned(re_lo, im_lo))
        e_ref[k, 0:128, :] = y[:, :128]
        e_ref[k, 128:256, :] = y[:, 128:]
        return carry

    lax.fori_loop(0, 16, second, 0, unroll=4)


AZIMUTH_SCRATCH = [
    pltpu.VMEM((16, 256, 128), F32),
    pltpu.VMEM((16, 8, 2, 16, 128), F32),
    pltpu.VMEM((16, 256, 256), BF16),
    pltpu.SemaphoreType.DMA((13,)),
]


def _azimuth_rows(e_ref, g):
    at = [pl.multiple_of(c * 128 + g * 8, 8) for c in range(2)]
    v = [(e_ref[k, pl.ds(at[0], 8), :], e_ref[k, pl.ds(at[1], 8), :]) for k in range(16)]
    return dft16(v, 1)


def _slave_kernel(x_hbm, a_hbm, left_hbm, right_hbm, left_ref, right_ref, *scratch):
    _azimuth_front(x_hbm, a_hbm, *scratch)
    e_ref, sem = scratch[0], scratch[-1]
    low = lax.broadcasted_iota(jnp.int32, (8, 128), 1) < 64
    zero = jnp.zeros((ASH, 128), F32)
    for ref in (left_ref, right_ref):
        ref[0:ASH, :] = zero
        ref[ASH + LINES :, :] = zero

    def third(g, carry):
        v = _azimuth_rows(e_ref, g)
        for a in range(16):
            rows = pl.ds(pl.multiple_of(a * 128 + g * 8 + ASH, 8), 8)
            r, i = v[a]
            left_ref[rows, :] = jnp.where(low, r, pltpu.roll(i, 64, 1))
            right_ref[rows, :] = jnp.where(low, pltpu.roll(r, 64, 1), i)
        return carry

    lax.fori_loop(0, 16, third, 0, unroll=2)
    copies = [
        pltpu.make_async_copy(right_ref, right_hbm, sem.at[10]),
        pltpu.make_async_copy(left_ref, left_hbm, sem.at[9]),
    ]
    for copy in copies:
        copy.start()
    for copy in copies:
        copy.wait()


def slave_azimuth(x, a):
    side = jax.ShapeDtypeStruct((LINES + 2 * ASH, 128), F32)
    return pl.pallas_call(
        _slave_kernel,
        in_specs=[HBM, HBM],
        out_specs=(HBM, HBM),
        out_shape=(side, side),
        scratch_shapes=[pltpu.VMEM(side.shape, F32)] * 2 + AZIMUTH_SCRATCH,
        cost_estimate=pl.CostEstimate(flops=5 * 10**9, bytes_accessed=10**7, transcendentals=0),
        compiler_params=limit(AZIMUTH_MIB),
        name="slave_azimuth",
    )(x.reshape(16, 8, 2, 16, 128), a)


def _master_kernel(x_hbm, a_hbm, o_hbm, o_ref, *scratch):
    _azimuth_front(x_hbm, a_hbm, *scratch)
    e_ref, sem = scratch[0], scratch[-1]

    def third(g, carry):
        v = _azimuth_rows(e_ref, g)
        for a in range(16):
            rows = pl.ds(pl.multiple_of(a * 128 + g * 8, 8), 8)
            o_ref[0, rows, :] = v[a][0]
            o_ref[1, rows, :] = v[a][1]
        return carry

    lax.fori_loop(0, 16, third, 0, unroll=2)
    copy = pltpu.make_async_copy(o_ref, o_hbm, sem.at[9])
    copy.start()
    copy.wait()


def master_azimuth(x, a):
    return pl.pallas_call(
        _master_kernel,
        in_specs=[HBM, HBM],
        out_specs=HBM,
        out_shape=jax.ShapeDtypeStruct((2, LINES, 128), F32),
        scratch_shapes=[pltpu.VMEM((2, LINES, 128), F32)] + AZIMUTH_SCRATCH,
        cost_estimate=pl.CostEstimate(flops=5 * 10**9, bytes_accessed=10**7, transcendentals=0),
        compiler_params=limit(MASTER_MIB),
        name="master_azimuth",
    )(x.reshape(16, 8, 2, 16, 128), a)


def _looks_kernel(shift_ref, *refs):
    packs, (m_hbm, n_ref, pick_ref, box_ref, side_ref) = refs[:4], refs[4:9]
    w_ref, m_ref, total_ref, sem = refs[9:]
    lane = lax.broadcasted_iota(jnp.int32, (64, 128), 1)
    line = lax.broadcasted_iota(jnp.int32, (64, 128), 0)
    low = lane < 64
    count = n_ref[...]

    def load(block):
        rows = pl.ds(0, BA + 2 * ASH) if block == 0 else pl.ds(block * BA + 2 * ASH, BA)
        mine = pl.ds(block * BA, BA)
        return [
            pltpu.make_async_copy(pack.at[rows], w_ref.at[k, rows], sem.at[5 * block + k])
            for k, pack in enumerate(packs)
        ] + [pltpu.make_async_copy(m_hbm.at[:, mine], m_ref.at[:, mine], sem.at[5 * block + 4])]

    for block in range(NBA):
        for copy in load(block):
            copy.start()
    for block in range(NBA):
        for copy in load(block):
            copy.wait()

        def move(t, carry):
            parts = []
            for r in range(2):
                shift = shift_ref[8 + 2 * block + r] + RSH
                first = shift // 64 + r
                second = jnp.minimum(first + 1, 3)
                s = lax.rem(shift, 64)
                rows = pl.ds(block * BA + t * 64 + ASH + shift_ref[2 * block + r], 64)
                parts.append(
                    jnp.where(
                        (lane & 63) + s < 64,
                        pltpu.roll(w_ref[first, rows, :], lax.rem(128 - s, 128), 1),
                        pltpu.roll(w_ref[second, rows, :], 64 - s, 1),
                    )
                )
            sr = jnp.where(low, parts[0], pltpu.roll(parts[1], 64, 1))
            si = jnp.where(low, pltpu.roll(parts[0], 64, 1), parts[1])
            at = pl.multiple_of(block * BA + t * 64, 64)
            r, i = m_ref[0, pl.ds(at, 64), :], m_ref[1, pl.ds(at, 64), :]
            keep = line + at < count
            cross = (r * sr + i * si, i * sr - r * si)
            for c in range(2):
                cells = jnp.where(keep, cross[c], 0.0).reshape(8, LOOK, 128).sum(axis=1)
                total_ref[pl.ds(pl.multiple_of(c * 256 + (block * 8 + t) * 8, 8), 8), :] = cells
            return carry

        lax.fori_loop(0, BA // 64, move, 0, unroll=4)
    y = _dot_t(pick_ref[...], total_ref[...])
    cell = lax.broadcasted_iota(jnp.int32, (24, 512), 1) % 256
    y = (
        y
        + jnp.where(cell == 0, 0.0, pltpu.roll(y, 1, 1))
        + jnp.where(cell == 255, 0.0, pltpu.roll(y, 511, 1))
    )
    box_ref[...] = y[:16]
    side_ref[...] = y[16:]


def looks(shifts, packs, master, counts):
    return pl.pallas_call(
        _looks_kernel,
        in_specs=[SMEM] + [HBM] * 5 + [VMEM] * 2,
        out_shape=(
            jax.ShapeDtypeStruct((16, 512), F32),
            jax.ShapeDtypeStruct((8, 512), F32),
        ),
        scratch_shapes=[
            pltpu.VMEM((4, LINES + 2 * ASH, 128), F32),
            pltpu.VMEM((2, LINES, 128), F32),
            pltpu.VMEM((512, 128), F32),
            pltpu.SemaphoreType.DMA((20,)),
        ],
        cost_estimate=pl.CostEstimate(flops=5 * 10**9, bytes_accessed=10**7, transcendentals=0),
        compiler_params=limit(61),
        name="looks",
    )(shifts, *packs, master, counts, TABLES["pick"])


def _final_kernel(box_ref, left_ref, right_ref, scale_ref, o_ref):
    row = lax.broadcasted_iota(jnp.int32, (16, 256), 0)
    for c in range(2):
        at = slice(256 * c, 256 * c + 256)
        x = box_ref[:, at]
        x = x + jnp.where(row == 0, left_ref[1:2, at], 0.0)
        x = x + jnp.where(row == 15, right_ref[0:1, at], 0.0)
        o_ref[c] = x * scale_ref[...]


def final(box, left, right, scale):
    return pl.pallas_call(
        _final_kernel,
        out_shape=jax.ShapeDtypeStruct((2, 16, 256), F32),
        compiler_params=limit(4),
        name="final",
    )(box, left, right, scale)


def to_worker(x):
    return lax.ppermute(x, ALL, [(b, worker(b)) for b in range(128)])


def halo(to_right, to_left):
    up = [(worker(b), worker(b + 1)) for b in range(127)]
    down = [(j, i) for i, j in up]
    return lax.ppermute(to_right, ALL, up), lax.ppermute(to_left, ALL, down)


def local(master_raw, slave_raw, range_ref, az_ref, az_shift, rg_shift, valid_lines):
    hf = range_ref.reshape(2, NS, NQ, NP).transpose(3, 2, 0, 1).reshape(NP * NQ, 2, NS)
    hf = jnp.pad(hf * (1.0 / RANGE), ((0, 0), (0, 0), (0, 3)))
    h = az_ref.reshape(2, 128, 16).transpose(0, 2, 1) * (1.0 / LINES)

    def columns_of(ranged):
        return lax.all_to_all(ranged, ALL, 0, 0, tiled=True)

    flat = lax.axis_index(ALL)
    counts = lax.dynamic_slice(jnp.pad(valid_lines, 1), (flat * 2,), (4,))
    wide = jnp.concatenate([counts[:1], jnp.repeat(counts[1:3], BR // LOOK), counts[3:]])
    rows = LINES // LOOK
    groups = lax.broadcasted_iota(jnp.int32, (18, rows + 2), 1) - 1
    pixels = jnp.clip(wide[:, None] - LOOK * groups, 0, LOOK) * LOOK
    pixels = jnp.where((groups >= 0) & (groups < rows), pixels, 0).astype(F32)
    box_pixels = sum(pixels[j : j + 16, i : i + rows] for i in range(3) for j in range(3))
    scale = 1.0 / jnp.sqrt(jnp.maximum(box_pixels, 1.0))
    block = block_of(lax.axis_index("az"), lax.axis_index("rg"))
    own = lax.dynamic_slice(valid_lines, (block * 2,), (2,))
    col_counts = jnp.repeat(own, BR)[None, :]
    shifts = to_worker(jnp.concatenate([az_shift.reshape(8), rg_shift.reshape(8)]))

    slave = pre(slave_raw)
    slave = lax.all_to_all(slave, "rg", 0, 0, tiled=True)
    me = lax.axis_index("rg").astype(jnp.int32)[None]
    pieces = pre_shifts(me, master_raw)
    master = [
        lax.ppermute(piece, "rg", [(r, shifted(r, shift)) for r in range(NP)])
        if any(shift)
        else piece
        for shift, piece in zip(SHIFTS, pieces)
    ]
    slave = range_compress(_range_kernel, [HBM], [slave], hf)
    slave = columns_of(slave)
    matrices = prep(h)
    master = range_compress(_range_shift_kernel, [SMEM] + [HBM] * NP, [me, *master], hf)
    master = columns_of(master)
    low, high = slave_azimuth(slave, matrices)
    from_left, from_right = halo(high, low)
    master = master_azimuth(master, matrices)
    box, side = looks(shifts, (from_left, low, high, from_right), master, col_counts)

    box = lax.ppermute(box, ALL, [(worker(b), b) for b in range(128)])
    left = lax.ppermute(side, ALL, [(worker(b), b + 1) for b in range(127)])
    right = lax.ppermute(side, ALL, [(worker(b + 1), b) for b in range(127)])
    return final(box, left, right, scale).transpose(0, 2, 1)


def solution(mesh):
    return jax.shard_map(
        local,
        mesh=mesh,
        in_specs=(
            P(None, "az", "rg"),
            P(None, "az", "rg"),
            P(),
            P(),
            P(None, ALL),
            P(None, ALL),
            P(),
        ),
        out_specs=P(None, None, ALL),
        check_vma=False,
    )
```

profile of v0, /device:TPU:1, one launch (start us, length us, event | category | flops | bytes accessed | tf_op | source)
XLA Modules:
  0.0 221.4 jit_solution(4108395993322404587)
XLA Ops:
  0.0 3.1 %pre.1 = f32[16,10,2,16,128]{4,3,2,1,0:T(8,128)} custom-call(f32[5000,128]{1,0:T(8,128)} %bitcast.22), custom_call_target="tpu_custom_call" | custom-call | flops 100000000 | bytes 10000000 | tf_op jit(solution)/shard_map/pre/pallas_call | solution.py:264
  3.1 8.6 %all-to-all-start = ((f32[16,10,2,16,128]{4,3,2,1,0:T(8,128)}), f32[16,10,2,16,128]{4,3,2,1,0:T(8,128)}, u32[]{:S(2)}, u32[]{:S(2)}) async-start(f32[16,10,2,16,128]{4,3,2,1,0:T(8,128)} %pre.1), calls=%async_computation | async-start | bytes 5242880 | tf_op jit(solution)/shard_map/all_to_all | solution.py:759
  14.0 36.8 %all-to-all-done.x_hbm = f32[16,10,2,16,128]{4,3,2,1,0:T(8,128)} async-done(((f32[16,10,2,16,128]{4,3,2,1,0:T(8,128)}), f32[16,10,2,16,128]{4,3,2,1,0:T(8,128)}, u32[]{:S(2)}, u32[]{:S(2)}) %all-to-all-start) | async-done | bytes 2621472 | tf_op jit(solution)/shard_map/all_to_all | solution.py:759
  50.9 8.7 %shard_map.163 = f32[128,2,16,128]{3,2,1,0:T(8,128)} custom-call(f32[16,10,2,16,128]{4,3,2,1,0:T(8,128)} %all-to-all-done.x_hbm, f32[10,2,128]{2,1,0:T(2,128)} %constant.106.clone.refs_0_.refs_16_, f32[160,2,128]{2,1,0:T(2,128)} %pad.8.refs_1_.refs_17_, bf16[256,256]{1,0:T(8,128)(2,1)} %constant.107.clone.refs_2_.refs_18_, ...), custom_call_target="tpu_custom_call" | custom-call | flops 10000000000 | bytes 6000000 | tf_op jit(solution)/shard_map/pallas_call | solution.py:430
  59.6 7.5 %all-to-all-start.1 = ((f32[128,2,16,128]{3,2,1,0:T(8,128)}), f32[128,2,16,128]{3,2,1,0:T(8,128)S(1)}, u32[]{:S(2)}, u32[]{:S(2)}) async-start(f32[128,2,16,128]{3,2,1,0:T(8,128)} %shard_map.163), calls=%async_computation.1 | async-start | bytes 4194304 | tf_op jit(solution)/shard_map/all_to_all | solution.py:742
  67.1 3.8 %pre_shifts.1 = (f32[10,2,16,128]{3,2,1,0:T(8,128)}, f32[10,2,16,128]{3,2,1,0:T(8,128)}, f32[10,2,16,128]{3,2,1,0:T(8,128)}, f32[10,2,16,128]{3,2,1,0:T(8,128)},...) custom-call(s32[1]{0:T(128)} %bitcast.8.me_ref, ...), custom_call_target="tpu_custom_call" | custom-call | flops 100000000 | bytes 10000000 | tf_op jit(solution)/shard_map/pre_shifts/pallas_call | solution.py:276
  70.9 4.2 %collective-permute-start.10 = (f32[10,2,16,128]{3,2,1,0:T(8,128)}, f32[10,2,16,128]{3,2,1,0:T(8,128)S(1)}, u32[]{:S(2)}, u32[]{:S(2)}) collective-permute-start(f32[10,2,16,128]{3,2,1,0:T(8,128)} %get-tuple-element.34), channel_id=1, source_target_pairs={{0,13},{1,14},{2,15},{3,12},{4,1},{5,2},{6,3},{7,0},{8,5},{9,6},{1... | collective-permute-start | bytes 491528 | tf_op jit(solution)/shard_map/ppermute | solution.py:763
  75.1 2.4 %collective-permute-start.11 = (f32[10,2,16,128]{3,2,1,0:T(8,128)}, f32[10,2,16,128]{3,2,1,0:T(8,128)S(1)}, u32[]{:S(2)}, u32[]{:S(2)}) collective-permute-start(f32[10,2,16,128]{3,2,1,0:T(8,128)} %get-tuple-element.35), channel_id=1, source_target_pairs={{0,2},{1,3},{2,0},{3,1},{4,6},{5,7},{6,4},{7,5},{8,10},{9,11},{10,... | collective-permute-start | bytes 491528 | tf_op jit(solution)/shard_map/ppermute | solution.py:763
  77.5 2.9 %collective-permute-start.13 = (f32[10,2,16,128]{3,2,1,0:T(8,128)}, f32[10,2,16,128]{3,2,1,0:T(8,128)S(1)}, u32[]{:S(2)}, u32[]{:S(2)}) collective-permute-start(f32[10,2,16,128]{3,2,1,0:T(8,128)} %get-tuple-element.37), channel_id=1, source_target_pairs={{0,15},{1,12},{2,13},{3,14},{4,3},{5,0},{6,1},{7,2},{8,7},{9,4},{1... | collective-permute-start | bytes 491528 | tf_op jit(solution)/shard_map/ppermute | solution.py:763
  80.5 16.9 %collective-permute-done.10.refs_7_ = f32[10,2,16,128]{3,2,1,0:T(8,128)S(1)} collective-permute-done((f32[10,2,16,128]{3,2,1,0:T(8,128)}, f32[10,2,16,128]{3,2,1,0:T(8,128)S(1)}, u32[]{:S(2)}, u32[]{:S(2)}) %collective-permute-start.10) | collective-permute-done | bytes 163872 | tf_op jit(solution)/shard_map/ppermute | solution.py:763
  98.9 2.0 collective-permute-done.11.refs_8_
  100.9 2.7 %collective-permute-start.17 = (f32[10,2,16,128]{3,2,1,0:T(8,128)}, f32[10,2,16,128]{3,2,1,0:T(8,128)S(1)}, u32[]{:S(2)}, u32[]{:S(2)}) collective-permute-start(f32[10,2,16,128]{3,2,1,0:T(8,128)} %get-tuple-element.41), channel_id=1, source_target_pairs={{0,3},{1,0},{2,1},{3,2},{4,7},{5,4},{6,5},{7,6},{8,11},{9,8},{10,9... | collective-permute-start | bytes 491528 | tf_op jit(solution)/shard_map/ppermute | solution.py:763
  103.6 4.1 %collective-permute-start.3 = (f32[10,2,16,128]{3,2,1,0:T(8,128)}, f32[10,2,16,128]{3,2,1,0:T(8,128)}, u32[]{:S(2)}, u32[]{:S(2)}) collective-permute-start(f32[10,2,16,128]{3,2,1,0:T(8,128)} %get-tuple-element.27), channel_id=1, source_target_pairs={{0,10},{1,11},{2,8},{3,9},{4,14},{5,15},{6,12},{7,13},{8,2},{9,3},... | collective-permute-start | bytes 491528 | tf_op jit(solution)/shard_map/ppermute | solution.py:763
  107.7 3.3 %collective-permute-start.5 = (f32[10,2,16,128]{3,2,1,0:T(8,128)}, f32[10,2,16,128]{3,2,1,0:T(8,128)}, u32[]{:S(2)}, u32[]{:S(2)}) collective-permute-start(f32[10,2,16,128]{3,2,1,0:T(8,128)} %get-tuple-element.29), channel_id=1, source_target_pairs={{0,6},{1,7},{2,4},{3,5},{4,10},{5,11},{6,8},{7,9},{8,14},{9,15},{1... | collective-permute-start | bytes 491528 | tf_op jit(solution)/shard_map/ppermute | solution.py:763
  112.8 4.3 %collective-permute-start.7 = (f32[10,2,16,128]{3,2,1,0:T(8,128)}, f32[10,2,16,128]{3,2,1,0:T(8,128)}, u32[]{:S(2)}, u32[]{:S(2)}) collective-permute-start(f32[10,2,16,128]{3,2,1,0:T(8,128)} %get-tuple-element.31), channel_id=1, source_target_pairs={{0,11},{1,8},{2,9},{3,10},{4,15},{5,12},{6,13},{7,14},{8,3},{9,0},... | collective-permute-start | bytes 491528 | tf_op jit(solution)/shard_map/ppermute | solution.py:763
  118.1 1.9 collective-permute-done.5.refs_2_
  120.1 2.9 %collective-permute-done.6.refs_3_ = f32[10,2,16,128]{3,2,1,0:T(8,128)} collective-permute-done((f32[10,2,16,128]{3,2,1,0:T(8,128)}, f32[10,2,16,128]{3,2,1,0:T(8,128)}, u32[]{:S(2)}, u32[]{:S(2)}) %collective-permute-start.6) | collective-permute-done | bytes 163872 | tf_op jit(solution)/shard_map/ppermute | solution.py:763
  123.0 2.5 %collective-permute-done.7.refs_4_ = f32[10,2,16,128]{3,2,1,0:T(8,128)} collective-permute-done((f32[10,2,16,128]{3,2,1,0:T(8,128)}, f32[10,2,16,128]{3,2,1,0:T(8,128)}, u32[]{:S(2)}, u32[]{:S(2)}) %collective-permute-start.7) | collective-permute-done | bytes 163872 | tf_op jit(solution)/shard_map/ppermute | solution.py:763
  125.4 9.8 %collective-permute-done.8.refs_5_ = f32[10,2,16,128]{3,2,1,0:T(8,128)} collective-permute-done((f32[10,2,16,128]{3,2,1,0:T(8,128)}, f32[10,2,16,128]{3,2,1,0:T(8,128)}, u32[]{:S(2)}, u32[]{:S(2)}) %collective-permute-start.8) | collective-permute-done | bytes 163872 | tf_op jit(solution)/shard_map/ppermute | solution.py:763
  135.3 9.6 %shard_map.164 = f32[128,2,16,128]{3,2,1,0:T(8,128)} custom-call(s32[1]{0:T(128)} %bitcast.8.me_ref, f32[10,2,16,128]{3,2,1,0:T(8,128)} %collective-permute-done.3.refs_0_, f32[10,2,16,128]{3,2,1,0:T(8,128)} %collective-permute-done.4.refs_1_, f32[10,2,16,128]{3,2,1,0:T(8,128)} %collective-permute-done.5.refs_2_, ...), custom_call_target="tpu_custom_call" | custom-call | flops 10000000000 | bytes 6000000 | tf_op jit(solution)/shard_map/pallas_call | solution.py:430
  146.4 5.3 %all-to-all-start.2 = ((f32[128,2,16,128]{3,2,1,0:T(8,128)}), f32[128,2,16,128]{3,2,1,0:T(8,128)S(1)}, u32[]{:S(2)}, u32[]{:S(2)}) async-start(f32[128,2,16,128]{3,2,1,0:T(8,128)} %shard_map.164), calls=%async_computation.2 | async-start | bytes 4194304 | tf_op jit(solution)/shard_map/all_to_all | solution.py:742
  152.1 5.0 %collective-permute-start = (s32[16]{0:T(128)S(1)}, s32[16]{0:T(128)S(1)}, u32[]{:S(2)}, u32[]{:S(2)}) collective-permute-start(s32[16]{0:T(128)S(1)} %pad_add_fusion), channel_id=1, source_target_pairs={{0,0},{1,16},{2,1},{3,17},{4,5},{5,21},{6,4},{7,20},{8,8},{9,24},{... | collective-permute-start | bytes 200 | tf_op jit(solution)/shard_map/ppermute | solution.py:727
  158.0 3.9 %prep.1.a_hbm = bf16[16,256,256]{2,1,0:T(8,128)(2,1)} custom-call(f32[2,16,128]{2,1,0:T(8,128)} %bitcast.27, f32[2,128,128]{2,1,0:T(8,128)} %constant.112.clone.dft_ref, f32[2,16,128]{2,1,0:T(8,128)} %constant.113.clone.turn_ref, f32[16,2,128]{2,1,0:T(2,128)} %constant.114.clone.wrap_ref), custom_call_target="tpu_custom_call" | custom-call | flops 2000000000 | bytes 5000000 | tf_op jit(solution)/shard_map/prep/pallas_call | solution.py:488
  161.9 6.5 %slave_azimuth.1 = (f32[2112,128]{1,0:T(8,128)}, f32[2112,128]{1,0:T(8,128)}) custom-call(f32[16,8,2,16,128]{4,3,2,1,0:T(8,128)} %bitcast.25, bf16[16,256,256]{2,1,0:T(8,128)(2,1)} %prep.1.a_hbm), custom_call_target="tpu_custom_call" | custom-call | flops 5000000000 | bytes 10000000 | tf_op jit(solution)/shard_map/slave_azimuth/pallas_call | solution.py:583
  168.4 1.9 collective-permute-start.1
  170.3 3.4 %collective-permute-start.2 = (f32[2112,128]{1,0:T(8,128)}, f32[2112,128]{1,0:T(8,128)}, u32[]{:S(2)}, u32[]{:S(2)}) collective-permute-start(f32[2112,128]{1,0:T(8,128)} %get-tuple-element.26.refs_1_), channel_id=1, source_target_pairs={{16,0},{1,16},{17,1},{5,17},{21,5},{4,21},{20,4},{8,20},{24,8},{9,... | collective-permute-start | bytes 3244040 | tf_op jit(solution)/shard_map/ppermute | solution.py:733
  176.9 4.4 %all-to-all-done.2 = f32[128,2,16,128]{3,2,1,0:T(8,128)S(1)} async-done(((f32[128,2,16,128]{3,2,1,0:T(8,128)}), f32[128,2,16,128]{3,2,1,0:T(8,128)S(1)}, u32[]{:S(2)}, u32[]{:S(2)}) %all-to-all-start.2) | async-done | bytes 2097184 | tf_op jit(solution)/shard_map/all_to_all | solution.py:742
  182.7 5.8 %master_azimuth.1.refs_4_ = f32[2,2048,128]{2,1,0:T(8,128)} custom-call(f32[16,8,2,16,128]{4,3,2,1,0:T(8,128)} %bitcast.24, bf16[16,256,256]{2,1,0:T(8,128)(2,1)} %prep.1.a_hbm), custom_call_target="tpu_custom_call" | custom-call | flops 5000000000 | bytes 10000000 | tf_op jit(solution)/shard_map/master_azimuth/pallas_call | solution.py:614
  189.1 6.3 %looks.1 = (f32[16,512]{1,0:T(8,128)}, f32[8,512]{1,0:T(8,128)}) custom-call(s32[16]{0:T(128)} %copy-done.15, f32[2112,128]{1,0:T(8,128)} %collective-permute-done.1.refs_0_, f32[2112,128]{1,0:T(8,128)} %get-tuple-element.26.refs_1_, f32[2112,128]{1,0:T(8,128)} %get-tuple-element.25.refs_2_, f32[2112,128]{1,0:T(8,128)} %collective-permute-done.2.refs_3_, ...), custom_call_target="tpu_custom_call" | custom-call | flops 5000000000 | bytes 10000000 | tf_op jit(solution)/shard_map/looks/pallas_call | solution.py:688
  195.4 16.5 %collective-permute-start.19 = (f32[8,512]{1,0:T(8,128)}, f32[8,512]{1,0:T(8,128)S(1)}, u32[]{:S(2)}, u32[]{:S(2)}) collective-permute-start(f32[8,512]{1,0:T(8,128)} %get-tuple-element.44), channel_id=1, source_target_pairs={{0,1},{16,2},{1,3},{17,4},{5,5},{21,6},{4,7},{20,8},{8,9},{24,10},... | collective-permute-start | bytes 49160 | tf_op jit(solution)/shard_map/ppermute | solution.py:779
  215.9 2.4 %collective-permute-done.20.right_ref = f32[8,512]{1,0:T(8,128)S(1)} collective-permute-done((f32[8,512]{1,0:T(8,128)}, f32[8,512]{1,0:T(8,128)S(1)}, u32[]{:S(2)}, u32[]{:S(2)}) %collective-permute-start.20) | collective-permute-done | bytes 16416 | tf_op jit(solution)/shard_map/ppermute | solution.py:780
  218.2 2.6 %collective-permute-done.18.box_ref = f32[16,512]{1,0:T(8,128)S(1)} collective-permute-done((f32[16,512]{1,0:T(8,128)}, f32[16,512]{1,0:T(8,128)S(1)}, u32[]{:S(2)}, u32[]{:S(2)}) %collective-permute-start.18) | collective-permute-done | bytes 32800 | tf_op jit(solution)/shard_map/ppermute | solution.py:778
  (82 shorter events, 19.0 us)
Async XLA Ops:
  3.1 47.7 %all-to-all-start = ((f32[16,10,2,16,128]{4,3,2,1,0:T(8,128)}), f32[16,10,2,16,128]{4,3,2,1,0:T(8,128)}, u32[]{:S(2)}, u32[]{:S(2)}) async-start(f32[16,10,2,16,128]{4,3,2,1,0:T(8,128)} %pre.1), calls=%async_computation | async-start | bytes 5242880 | tf_op jit(solution)/shard_map/all_to_all | solution.py:759
  59.6 85.4 %all-to-all-start.1 = ((f32[128,2,16,128]{3,2,1,0:T(8,128)}), f32[128,2,16,128]{3,2,1,0:T(8,128)S(1)}, u32[]{:S(2)}, u32[]{:S(2)}) async-start(f32[128,2,16,128]{3,2,1,0:T(8,128)} %shard_map.163), calls=%async_computation.1 | async-start | bytes 4194304 | tf_op jit(solution)/shard_map/all_to_all | solution.py:742
  70.9 26.4 %collective-permute-start.10 = (f32[10,2,16,128]{3,2,1,0:T(8,128)}, f32[10,2,16,128]{3,2,1,0:T(8,128)S(1)}, u32[]{:S(2)}, u32[]{:S(2)}) collective-permute-start(f32[10,2,16,128]{3,2,1,0:T(8,128)} %get-tuple-element.34), channel_id=1, source_target_pairs={{0,13},{1,14},{2,15},{3,12},{4,1},{5,2},{6,3},{7,0},{8,5},{9,6},{1... | collective-permute-start | bytes 491528 | tf_op jit(solution)/shard_map/ppermute | solution.py:763
  75.1 25.7 %collective-permute-start.11 = (f32[10,2,16,128]{3,2,1,0:T(8,128)}, f32[10,2,16,128]{3,2,1,0:T(8,128)S(1)}, u32[]{:S(2)}, u32[]{:S(2)}) collective-permute-start(f32[10,2,16,128]{3,2,1,0:T(8,128)} %get-tuple-element.35), channel_id=1, source_target_pairs={{0,2},{1,3},{2,0},{3,1},{4,6},{5,7},{6,4},{7,5},{8,10},{9,11},{10,... | collective-permute-start | bytes 491528 | tf_op jit(solution)/shard_map/ppermute | solution.py:763
  77.5 23.3 %collective-permute-start.12 = (f32[10,2,16,128]{3,2,1,0:T(8,128)}, f32[10,2,16,128]{3,2,1,0:T(8,128)S(1)}, u32[]{:S(2)}, u32[]{:S(2)}) collective-permute-start(f32[10,2,16,128]{3,2,1,0:T(8,128)} %get-tuple-element.36), channel_id=1, source_target_pairs={{0,7},{1,4},{2,5},{3,6},{4,11},{5,8},{6,9},{7,10},{8,15},{9,12},{1... | collective-permute-start | bytes 491528 | tf_op jit(solution)/shard_map/ppermute | solution.py:763
  77.5 26.0 %collective-permute-start.13 = (f32[10,2,16,128]{3,2,1,0:T(8,128)}, f32[10,2,16,128]{3,2,1,0:T(8,128)S(1)}, u32[]{:S(2)}, u32[]{:S(2)}) collective-permute-start(f32[10,2,16,128]{3,2,1,0:T(8,128)} %get-tuple-element.37), channel_id=1, source_target_pairs={{0,15},{1,12},{2,13},{3,14},{4,3},{5,0},{6,1},{7,2},{8,7},{9,4},{1... | collective-permute-start | bytes 491528 | tf_op jit(solution)/shard_map/ppermute | solution.py:763
  80.5 27.2 %collective-permute-start.14 = (f32[10,2,16,128]{3,2,1,0:T(8,128)}, f32[10,2,16,128]{3,2,1,0:T(8,128)S(1)}, u32[]{:S(2)}, u32[]{:S(2)}) collective-permute-start(f32[10,2,16,128]{3,2,1,0:T(8,128)} %get-tuple-element.38), channel_id=1, source_target_pairs={{0,4},{1,5},{2,6},{3,7},{4,8},{5,9},{6,10},{7,11},{8,12},{9,13},{1... | collective-permute-start | bytes 491528 | tf_op jit(solution)/shard_map/ppermute | solution.py:763
  97.3 37.9 %copy-start.7 = (f32[10,2,16,128]{3,2,1,0:T(8,128)}, f32[10,2,16,128]{3,2,1,0:T(8,128)S(1)}, u32[]{:S(2)}) copy-start(f32[10,2,16,128]{3,2,1,0:T(8,128)S(1)} %collective-permute-done.10.refs_7_) | copy-start | bytes 491524
  97.3 10.3 %collective-permute-start.15 = (f32[10,2,16,128]{3,2,1,0:T(8,128)}, f32[10,2,16,128]{3,2,1,0:T(8,128)S(1)}, u32[]{:S(2)}, u32[]{:S(2)}) collective-permute-start(f32[10,2,16,128]{3,2,1,0:T(8,128)} %get-tuple-element.39), channel_id=1, source_target_pairs={{0,12},{1,13},{2,14},{3,15},{4,0},{5,1},{6,2},{7,3},{8,4},{9,5},{1... | collective-permute-start | bytes 491528 | tf_op jit(solution)/shard_map/ppermute | solution.py:763
  100.9 34.4 %copy-start.8 = (f32[10,2,16,128]{3,2,1,0:T(8,128)}, f32[10,2,16,128]{3,2,1,0:T(8,128)S(1)}, u32[]{:S(2)}) copy-start(f32[10,2,16,128]{3,2,1,0:T(8,128)S(1)} %collective-permute-done.11.refs_8_) | copy-start | bytes 491524
  100.9 10.1 %collective-permute-start.16 = (f32[10,2,16,128]{3,2,1,0:T(8,128)}, f32[10,2,16,128]{3,2,1,0:T(8,128)S(1)}, u32[]{:S(2)}, u32[]{:S(2)}) collective-permute-start(f32[10,2,16,128]{3,2,1,0:T(8,128)} %get-tuple-element.40), channel_id=1, source_target_pairs={{0,1},{1,2},{2,3},{3,0},{4,5},{5,6},{6,7},{7,4},{8,9},{9,10},{10,1... | collective-permute-start | bytes 491528 | tf_op jit(solution)/shard_map/ppermute | solution.py:763
  100.9 34.4 %copy-start.9 = (f32[10,2,16,128]{3,2,1,0:T(8,128)}, f32[10,2,16,128]{3,2,1,0:T(8,128)S(1)}, u32[]{:S(2)}) copy-start(f32[10,2,16,128]{3,2,1,0:T(8,128)S(1)} %collective-permute-done.12.refs_9_) | copy-start | bytes 491524
  100.9 12.0 %collective-permute-start.17 = (f32[10,2,16,128]{3,2,1,0:T(8,128)}, f32[10,2,16,128]{3,2,1,0:T(8,128)S(1)}, u32[]{:S(2)}, u32[]{:S(2)}) collective-permute-start(f32[10,2,16,128]{3,2,1,0:T(8,128)} %get-tuple-element.41), channel_id=1, source_target_pairs={{0,3},{1,0},{2,1},{3,2},{4,7},{5,4},{6,5},{7,6},{8,11},{9,8},{10,9... | collective-permute-start | bytes 491528 | tf_op jit(solution)/shard_map/ppermute | solution.py:763
  103.5 31.7 %copy-start.10 = (f32[10,2,16,128]{3,2,1,0:T(8,128)}, f32[10,2,16,128]{3,2,1,0:T(8,128)S(1)}, u32[]{:S(2)}) copy-start(f32[10,2,16,128]{3,2,1,0:T(8,128)S(1)} %collective-permute-done.13.refs_10_) | copy-start | bytes 491524
  103.6 13.6 %collective-permute-start.3 = (f32[10,2,16,128]{3,2,1,0:T(8,128)}, f32[10,2,16,128]{3,2,1,0:T(8,128)}, u32[]{:S(2)}, u32[]{:S(2)}) collective-permute-start(f32[10,2,16,128]{3,2,1,0:T(8,128)} %get-tuple-element.27), channel_id=1, source_target_pairs={{0,10},{1,11},{2,8},{3,9},{4,14},{5,15},{6,12},{7,13},{8,2},{9,3},... | collective-permute-start | bytes 491528 | tf_op jit(solution)/shard_map/ppermute | solution.py:763
  107.6 27.6 %copy-start.11 = (f32[10,2,16,128]{3,2,1,0:T(8,128)}, f32[10,2,16,128]{3,2,1,0:T(8,128)S(1)}, u32[]{:S(2)}) copy-start(f32[10,2,16,128]{3,2,1,0:T(8,128)S(1)} %collective-permute-done.14.refs_11_) | copy-start | bytes 491524
  107.6 10.5 %collective-permute-start.4 = (f32[10,2,16,128]{3,2,1,0:T(8,128)}, f32[10,2,16,128]{3,2,1,0:T(8,128)}, u32[]{:S(2)}, u32[]{:S(2)}) collective-permute-start(f32[10,2,16,128]{3,2,1,0:T(8,128)} %get-tuple-element.28), channel_id=1, source_target_pairs={{0,9},{1,10},{2,11},{3,8},{4,13},{5,14},{6,15},{7,12},{8,1},{9,2},... | collective-permute-start | bytes 491528 | tf_op jit(solution)/shard_map/ppermute | solution.py:763
  107.7 27.6 %copy-start.12 = (f32[10,2,16,128]{3,2,1,0:T(8,128)}, f32[10,2,16,128]{3,2,1,0:T(8,128)S(1)}, u32[]{:S(2)}) copy-start(f32[10,2,16,128]{3,2,1,0:T(8,128)S(1)} %collective-permute-done.15.refs_12_) | copy-start | bytes 491524
  107.7 12.4 %collective-permute-start.5 = (f32[10,2,16,128]{3,2,1,0:T(8,128)}, f32[10,2,16,128]{3,2,1,0:T(8,128)}, u32[]{:S(2)}, u32[]{:S(2)}) collective-permute-start(f32[10,2,16,128]{3,2,1,0:T(8,128)} %get-tuple-element.29), channel_id=1, source_target_pairs={{0,6},{1,7},{2,4},{3,5},{4,10},{5,11},{6,8},{7,9},{8,14},{9,15},{1... | collective-permute-start | bytes 491528 | tf_op jit(solution)/shard_map/ppermute | solution.py:763
  111.0 24.3 %copy-start.13 = (f32[10,2,16,128]{3,2,1,0:T(8,128)}, f32[10,2,16,128]{3,2,1,0:T(8,128)S(1)}, u32[]{:S(2)}) copy-start(f32[10,2,16,128]{3,2,1,0:T(8,128)S(1)} %collective-permute-done.16.refs_13_) | copy-start | bytes 491524
  111.0 12.0 %collective-permute-start.6 = (f32[10,2,16,128]{3,2,1,0:T(8,128)}, f32[10,2,16,128]{3,2,1,0:T(8,128)}, u32[]{:S(2)}, u32[]{:S(2)}) collective-permute-start(f32[10,2,16,128]{3,2,1,0:T(8,128)} %get-tuple-element.30), channel_id=1, source_target_pairs={{0,14},{1,15},{2,12},{3,13},{4,2},{5,3},{6,0},{7,1},{8,6},{9,7},{1... | collective-permute-start | bytes 491528 | tf_op jit(solution)/shard_map/ppermute | solution.py:763
  112.8 22.5 %copy-start.14 = (f32[10,2,16,128]{3,2,1,0:T(8,128)}, f32[10,2,16,128]{3,2,1,0:T(8,128)S(1)}, u32[]{:S(2)}) copy-start(f32[10,2,16,128]{3,2,1,0:T(8,128)S(1)} %collective-permute-done.17.refs_14_) | copy-start | bytes 491524
  112.8 12.6 %collective-permute-start.7 = (f32[10,2,16,128]{3,2,1,0:T(8,128)}, f32[10,2,16,128]{3,2,1,0:T(8,128)}, u32[]{:S(2)}, u32[]{:S(2)}) collective-permute-start(f32[10,2,16,128]{3,2,1,0:T(8,128)} %get-tuple-element.31), channel_id=1, source_target_pairs={{0,11},{1,8},{2,9},{3,10},{4,15},{5,12},{6,13},{7,14},{8,3},{9,0},... | collective-permute-start | bytes 491528 | tf_op jit(solution)/shard_map/ppermute | solution.py:763
  117.2 18.1 %collective-permute-start.8 = (f32[10,2,16,128]{3,2,1,0:T(8,128)}, f32[10,2,16,128]{3,2,1,0:T(8,128)}, u32[]{:S(2)}, u32[]{:S(2)}) collective-permute-start(f32[10,2,16,128]{3,2,1,0:T(8,128)} %get-tuple-element.32), channel_id=1, source_target_pairs={{0,8},{1,9},{2,10},{3,11},{4,12},{5,13},{6,14},{7,15},{8,0},{9,1},... | collective-permute-start | bytes 491528 | tf_op jit(solution)/shard_map/ppermute | solution.py:763
  118.1 17.1 %collective-permute-start.9 = (f32[10,2,16,128]{3,2,1,0:T(8,128)}, f32[10,2,16,128]{3,2,1,0:T(8,128)}, u32[]{:S(2)}, u32[]{:S(2)}) collective-permute-start(f32[10,2,16,128]{3,2,1,0:T(8,128)} %get-tuple-element.33), channel_id=1, source_target_pairs={{0,5},{1,6},{2,7},{3,4},{4,9},{5,10},{6,11},{7,8},{8,13},{9,14},{1... | collective-permute-start | bytes 491528 | tf_op jit(solution)/shard_map/ppermute | solution.py:763
  146.4 34.9 %all-to-all-start.2 = ((f32[128,2,16,128]{3,2,1,0:T(8,128)}), f32[128,2,16,128]{3,2,1,0:T(8,128)S(1)}, u32[]{:S(2)}, u32[]{:S(2)}) async-start(f32[128,2,16,128]{3,2,1,0:T(8,128)} %shard_map.164), calls=%async_computation.2 | async-start | bytes 4194304 | tf_op jit(solution)/shard_map/all_to_all | solution.py:742
  152.1 36.3 %collective-permute-start = (s32[16]{0:T(128)S(1)}, s32[16]{0:T(128)S(1)}, u32[]{:S(2)}, u32[]{:S(2)}) collective-permute-start(s32[16]{0:T(128)S(1)} %pad_add_fusion), channel_id=1, source_target_pairs={{0,0},{1,16},{2,1},{3,17},{4,5},{5,21},{6,4},{7,20},{8,8},{9,24},{... | collective-permute-start | bytes 200 | tf_op jit(solution)/shard_map/ppermute | solution.py:727
  168.4 20.1 %collective-permute-start.1 = (f32[2112,128]{1,0:T(8,128)}, f32[2112,128]{1,0:T(8,128)}, u32[]{:S(2)}, u32[]{:S(2)}) collective-permute-start(f32[2112,128]{1,0:T(8,128)} %get-tuple-element.25.refs_2_), channel_id=1, source_target_pairs={{0,16},{16,1},{1,17},{17,5},{5,21},{21,4},{4,20},{20,8},{8,24},{24... | collective-permute-start | bytes 3244040 | tf_op jit(solution)/shard_map/ppermute | solution.py:733
  170.3 18.2 %collective-permute-start.2 = (f32[2112,128]{1,0:T(8,128)}, f32[2112,128]{1,0:T(8,128)}, u32[]{:S(2)}, u32[]{:S(2)}) collective-permute-start(f32[2112,128]{1,0:T(8,128)} %get-tuple-element.26.refs_1_), channel_id=1, source_target_pairs={{16,0},{1,16},{17,1},{5,17},{21,5},{4,21},{20,4},{8,20},{24,8},{9,... | collective-permute-start | bytes 3244040 | tf_op jit(solution)/shard_map/ppermute | solution.py:733
  195.4 20.5 %collective-permute-start.19 = (f32[8,512]{1,0:T(8,128)}, f32[8,512]{1,0:T(8,128)S(1)}, u32[]{:S(2)}, u32[]{:S(2)}) collective-permute-start(f32[8,512]{1,0:T(8,128)} %get-tuple-element.44), channel_id=1, source_target_pairs={{0,1},{16,2},{1,3},{17,4},{5,5},{21,6},{4,7},{20,8},{8,9},{24,10},... | collective-permute-start | bytes 49160 | tf_op jit(solution)/shard_map/ppermute | solution.py:779
  211.9 6.3 %collective-permute-start.20 = (f32[8,512]{1,0:T(8,128)}, f32[8,512]{1,0:T(8,128)S(1)}, u32[]{:S(2)}, u32[]{:S(2)}) collective-permute-start(f32[8,512]{1,0:T(8,128)} %get-tuple-element.44), channel_id=1, source_target_pairs={{16,0},{1,1},{17,2},{5,3},{21,4},{4,5},{20,6},{8,7},{24,8},{9,9},{... | collective-permute-start | bytes 49160 | tf_op jit(solution)/shard_map/ppermute | solution.py:780
  213.8 6.9 %collective-permute-start.18 = (f32[16,512]{1,0:T(8,128)}, f32[16,512]{1,0:T(8,128)S(1)}, u32[]{:S(2)}, u32[]{:S(2)}) collective-permute-start(f32[16,512]{1,0:T(8,128)} %get-tuple-element.43), channel_id=1, source_target_pairs={{0,0},{16,1},{1,2},{17,3},{5,4},{21,5},{4,6},{20,7},{8,8},{24,9},{... | collective-permute-start | bytes 98312 | tf_op jit(solution)/shard_map/ppermute | solution.py:778
  (8 other events, 49.7 us)
where the time goes:
time: 222 us; the launch traced here: 221 us
  waiting for transfers between devices  82.3 us (37%)
  starting transfers between devices  80.2 us (36%)
  Pallas kernels  48.3 us (22%)
  local copies, waits for them, and re-layouts  8.44 us (4%)
    all_to_all x1, waiting for transfers between devices, local(): slave = lax.all_to_all(slave, 'rg', 0, 0, tiled=True)  36.8 us
    ppermute x15, waiting for transfers between devices, local(): lax.ppermute(piece, 'rg', [(r, shifted(r, shift)) for r in range(NP)])  36.2 us
    ppermute x15, starting transfers between devices, local(): lax.ppermute(piece, 'rg', [(r, shifted(r, shift)) for r in range(NP)])  28.1 us
    pallas_call x2, Pallas kernels, range_compress(): pl.pallas_call(kernel, in_specs=specs + [HBM] * 7, out_specs=HBM, out_sha...  18.3 us
    ppermute x1, starting transfers between devices, local(): left = lax.ppermute(side, ALL, [(worker(b), b + 1) for b in range(127)])  16.5 us
    all_to_all x2, starting transfers between devices, columns_of(): return lax.all_to_all(ranged, ALL, 0, 0, tiled=True)  12.8 us
    all_to_all x1, starting transfers between devices, local(): slave = lax.all_to_all(slave, 'rg', 0, 0, tiled=True)  8.6 us
    pallas_call x1, Pallas kernels, slave_azimuth(): pl.pallas_call(_slave_kernel, in_specs=[HBM, HBM], out_specs=(HBM, HBM),...  6.46 us
  transfers between devices with their start and end apart: 24, of which 11 were waited for; matrix products, arithmetic and copies ran while one was open for 3% of the time, Pallas kernels for 13%

commit v1 on v0

--- a/solution.py
+++ b/solution.py
@@ -141,13 +141,17 @@
     c, rest = divmod(rest, 16)
     z, x = divmod(rest, 4)
     pair, core = divmod(x, 2)
-    return (y * 2 + core) * 16 + z * 4 + 2 * c + (pair + z) % 2
+    turn = (pair + z) % 2
+    return (y * 2 + core) * 16 + (3 - z if c else z) * 4 + (3 - turn if c else turn)
 
 
 def block_of(az, rg):
     y, core = az // 2, az % 2
     z, x = rg // 4, rg % 4
-    return y * 32 + (x // 2) * 16 + z * 4 + 2 * ((x + z) % 2) + core
+    c = x // 2
+    z = z + c * (3 - 2 * z)
+    turn = x + c * (3 - 2 * x)
+    return y * 32 + c * 16 + z * 4 + 2 * ((turn + z) % 2) + core
 
 
 def _np_split(x):
@@ -197,8 +201,8 @@
 SMEM = pl.BlockSpec(memory_space=pltpu.SMEM)
 
 
-AZIMUTH_MIB = 61
-MASTER_MIB = 61
+AZIMUTH_MIB = 48
+MASTER_MIB = 52
 
 
 def limit(mib):
@@ -332,7 +336,7 @@
             d_ref[at, 1] = i
         return carry
 
-    lax.fori_loop(0, NP, middle, 0, unroll=4)
+    lax.fori_loop(0, NP, middle, 0, unroll=8)
 
     def inner(q, carry):
         for g in range(2):
@@ -494,17 +498,22 @@
     )(h, t["dft"], t["turn"], t["wrap"])
 
 
-def _azimuth_front(x_hbm, a_hbm, e_ref, x_ref, a_ref, sem):
+def _azimuth_front(x_hbm, a_hbm, e_ref, a_ref, sem, x_ref=None):
     def load(s):
         return pltpu.make_async_copy(x_hbm.at[:, s], x_ref.at[:, s], sem.at[s])
 
     matrices = pltpu.make_async_copy(a_hbm, a_ref, sem.at[8])
-    for s in range(8):
-        load(s).start()
+    staged = x_ref is not None
+    if staged:
+        for s in range(8):
+            load(s).start()
+    else:
+        x_ref = x_hbm
     matrices.start()
 
     def first(s, carry):
-        load(s).wait()
+        if staged:
+            load(s).wait()
         for g in range(2):
             rows = slice(8 * g, 8 * g + 8)
             v = [(x_ref[a, s, 0, rows, :], x_ref[a, s, 1, rows, :]) for a in range(16)]
@@ -537,10 +546,10 @@
 
 AZIMUTH_SCRATCH = [
     pltpu.VMEM((16, 256, 128), F32),
-    pltpu.VMEM((16, 8, 2, 16, 128), F32),
     pltpu.VMEM((16, 256, 256), BF16),
     pltpu.SemaphoreType.DMA((13,)),
 ]
+STAGED_SCRATCH = AZIMUTH_SCRATCH + [pltpu.VMEM((16, 8, 2, 16, 128), F32)]
 
 
 def _azimuth_rows(e_ref, g):
@@ -549,9 +558,9 @@
     return dft16(v, 1)
 
 
-def _slave_kernel(x_hbm, a_hbm, left_hbm, right_hbm, left_ref, right_ref, *scratch):
-    _azimuth_front(x_hbm, a_hbm, *scratch)
-    e_ref, sem = scratch[0], scratch[-1]
+def _slave_kernel(x_ref, a_hbm, left_hbm, right_hbm, left_ref, right_ref, *scratch):
+    _azimuth_front(x_ref, a_hbm, *scratch)
+    e_ref, sem = scratch[0], scratch[2]
     low = lax.broadcasted_iota(jnp.int32, (8, 128), 1) < 64
     zero = jnp.zeros((ASH, 128), F32)
     for ref in (left_ref, right_ref):
@@ -582,7 +591,7 @@
     side = jax.ShapeDtypeStruct((LINES + 2 * ASH, 128), F32)
     return pl.pallas_call(
         _slave_kernel,
-        in_specs=[HBM, HBM],
+        in_specs=[VMEM, HBM],
         out_specs=(HBM, HBM),
         out_shape=(side, side),
         scratch_shapes=[pltpu.VMEM(side.shape, F32)] * 2 + AZIMUTH_SCRATCH,
@@ -594,7 +603,7 @@
 
 def _master_kernel(x_hbm, a_hbm, o_hbm, o_ref, *scratch):
     _azimuth_front(x_hbm, a_hbm, *scratch)
-    e_ref, sem = scratch[0], scratch[-1]
+    e_ref, sem = scratch[0], scratch[2]
 
     def third(g, carry):
         v = _azimuth_rows(e_ref, g)
@@ -616,7 +625,7 @@
         in_specs=[HBM, HBM],
         out_specs=HBM,
         out_shape=jax.ShapeDtypeStruct((2, LINES, 128), F32),
-        scratch_shapes=[pltpu.VMEM((2, LINES, 128), F32)] + AZIMUTH_SCRATCH,
+        scratch_shapes=[pltpu.VMEM((2, LINES, 128), F32)] + STAGED_SCRATCH,
         cost_estimate=pl.CostEstimate(flops=5 * 10**9, bytes_accessed=10**7, transcendentals=0),
         compiler_params=limit(MASTER_MIB),
         name="master_azimuth",
@@ -699,7 +708,7 @@
             pltpu.SemaphoreType.DMA((20,)),
         ],
         cost_estimate=pl.CostEstimate(flops=5 * 10**9, bytes_accessed=10**7, transcendentals=0),
-        compiler_params=limit(61),
+        compiler_params=limit(50),
         name="looks",
     )(shifts, *packs, master, counts, TABLES["pick"])
 

time: 222 us -> 209 us (0.941)
  starting transfers between devices: 80.2 us -> 70.9 us
  local copies, waits for them, and re-layouts: 8.44 us -> 4.52 us
  waiting for transfers between devices: 82.3 us -> 85.2 us
  Pallas kernels: 48.3 us -> 45.6 us
    ppermute x1, starting transfers between devices: 16.5 us -> 5.1 us  [local(): left = lax.ppermute(side, ALL, [(worker(b), b + 1) for b in range(127)])]
    unnamed x34 -> x30, local copies, waits for them, and re-layouts: 3.53 us -> 0.25 us
    ppermute x1, starting transfers between devices: 5.04 us -> 7.56 us  [to_worker(): return lax.ppermute(x, ALL, [(b, worker(b)) for b in range(128)])]
  transfers between devices with their start and end apart: 24 -> 24, of which waited for: 11 -> 12; matrix products, arithmetic and copies ran while one was open for 3% -> 3% of each run, Pallas kernels for 13% -> 13%
where the time goes in v1:
time: 209 us; the launch traced here: 208 us
  waiting for transfers between devices  85.2 us (41%)
  starting transfers between devices  70.9 us (34%)
  Pallas kernels  45.6 us (22%)
  local copies, waits for them, and re-layouts  4.52 us (2%)
    all_to_all x1, waiting for transfers between devices, local(): slave = lax.all_to_all(slave, 'rg', 0, 0, tiled=True)  36.9 us
    ppermute x15, waiting for transfers between devices, local(): lax.ppermute(piece, 'rg', [(r, shifted(r, shift)) for r in range(NP)])  36.2 us
    ppermute x15, starting transfers between devices, local(): lax.ppermute(piece, 'rg', [(r, shifted(r, shift)) for r in range(NP)])  28.1 us
    pallas_call x2, Pallas kernels, range_compress(): pl.pallas_call(kernel, in_specs=specs + [HBM] * 7, out_specs=HBM, out_sha...  17.4 us
    all_to_all x2, starting transfers between devices, columns_of(): return lax.all_to_all(ranged, ALL, 0, 0, tiled=True)  13.3 us
    all_to_all x1, starting transfers between devices, local(): slave = lax.all_to_all(slave, 'rg', 0, 0, tiled=True)  8.6 us
    ppermute x1, starting transfers between devices, to_worker(): return lax.ppermute(x, ALL, [(b, worker(b)) for b in range(128)])  7.56 us
    pallas_call x1, Pallas kernels, master_azimuth(): pl.pallas_call(_master_kernel, in_specs=[HBM, HBM], out_specs=HBM, out_sh...  5.81 us
  transfers between devices with their start and end apart: 24, of which 12 were waited for; matrix products, arithmetic and copies ran while one was open for 3% of the time, Pallas kernels for 13%

profile of v1, /device:TPU:1, one launch (start us, length us, event | category | flops | bytes accessed | tf_op | source)
XLA Modules:
  0.0 208.3 jit_solution(14634988506524092318)
XLA Ops:
  0.0 3.1 %pre.1 = f32[16,10,2,16,128]{4,3,2,1,0:T(8,128)} custom-call(f32[5000,128]{1,0:T(8,128)} %bitcast.23), custom_call_target="tpu_custom_call" | custom-call | flops 100000000 | bytes 10000000 | tf_op jit(solution)/shard_map/pre/pallas_call | solution.py:268
  3.2 8.6 %all-to-all-start = ((f32[16,10,2,16,128]{4,3,2,1,0:T(8,128)}), f32[16,10,2,16,128]{4,3,2,1,0:T(8,128)}, u32[]{:S(2)}, u32[]{:S(2)}) async-start(f32[16,10,2,16,128]{4,3,2,1,0:T(8,128)} %pre.1), calls=%async_computation | async-start | bytes 5242880 | tf_op jit(solution)/shard_map/all_to_all | solution.py:768
  14.0 36.9 %all-to-all-done.x_hbm = f32[16,10,2,16,128]{4,3,2,1,0:T(8,128)} async-done(((f32[16,10,2,16,128]{4,3,2,1,0:T(8,128)}), f32[16,10,2,16,128]{4,3,2,1,0:T(8,128)}, u32[]{:S(2)}, u32[]{:S(2)}) %all-to-all-start) | async-done | bytes 2621472 | tf_op jit(solution)/shard_map/all_to_all | solution.py:768
  50.9 8.3 %shard_map.163 = f32[128,2,16,128]{3,2,1,0:T(8,128)} custom-call(f32[16,10,2,16,128]{4,3,2,1,0:T(8,128)} %all-to-all-done.x_hbm, f32[10,2,128]{2,1,0:T(2,128)} %constant.107.clone.refs_0_.refs_16_, f32[160,2,128]{2,1,0:T(2,128)} %pad.8.refs_1_.refs_17_, bf16[256,256]{1,0:T(8,128)(2,1)} %constant.108.clone.refs_2_.refs_18_, ...), custom_call_target="tpu_custom_call" | custom-call | flops 10000000000 | bytes 6000000 | tf_op jit(solution)/shard_map/pallas_call | solution.py:434
  59.2 7.5 %all-to-all-start.1 = ((f32[128,2,16,128]{3,2,1,0:T(8,128)}), f32[128,2,16,128]{3,2,1,0:T(8,128)S(1)}, u32[]{:S(2)}, u32[]{:S(2)}) async-start(f32[128,2,16,128]{3,2,1,0:T(8,128)} %shard_map.163), calls=%async_computation.1 | async-start | bytes 4194304 | tf_op jit(solution)/shard_map/all_to_all | solution.py:751
  66.7 3.8 %pre_shifts.1 = (f32[10,2,16,128]{3,2,1,0:T(8,128)}, f32[10,2,16,128]{3,2,1,0:T(8,128)}, f32[10,2,16,128]{3,2,1,0:T(8,128)}, f32[10,2,16,128]{3,2,1,0:T(8,128)},...) custom-call(s32[1]{0:T(128)} %bitcast.8.me_ref, ...), custom_call_target="tpu_custom_call" | custom-call | flops 100000000 | bytes 10000000 | tf_op jit(solution)/shard_map/pre_shifts/pallas_call | solution.py:280
  70.5 4.2 %collective-permute-start.10 = (f32[10,2,16,128]{3,2,1,0:T(8,128)}, f32[10,2,16,128]{3,2,1,0:T(8,128)S(1)}, u32[]{:S(2)}, u32[]{:S(2)}) collective-permute-start(f32[10,2,16,128]{3,2,1,0:T(8,128)} %get-tuple-element.34), channel_id=1, source_target_pairs={{0,13},{1,14},{2,15},{3,12},{4,1},{5,2},{6,3},{7,0},{8,5},{9,6},{1... | collective-permute-start | bytes 491528 | tf_op jit(solution)/shard_map/ppermute | solution.py:772
  74.7 2.4 %collective-permute-start.11 = (f32[10,2,16,128]{3,2,1,0:T(8,128)}, f32[10,2,16,128]{3,2,1,0:T(8,128)S(1)}, u32[]{:S(2)}, u32[]{:S(2)}) collective-permute-start(f32[10,2,16,128]{3,2,1,0:T(8,128)} %get-tuple-element.35), channel_id=1, source_target_pairs={{0,2},{1,3},{2,0},{3,1},{4,6},{5,7},{6,4},{7,5},{8,10},{9,11},{10,... | collective-permute-start | bytes 491528 | tf_op jit(solution)/shard_map/ppermute | solution.py:772
  77.1 2.9 %collective-permute-start.13 = (f32[10,2,16,128]{3,2,1,0:T(8,128)}, f32[10,2,16,128]{3,2,1,0:T(8,128)S(1)}, u32[]{:S(2)}, u32[]{:S(2)}) collective-permute-start(f32[10,2,16,128]{3,2,1,0:T(8,128)} %get-tuple-element.37), channel_id=1, source_target_pairs={{0,15},{1,12},{2,13},{3,14},{4,3},{5,0},{6,1},{7,2},{8,7},{9,4},{1... | collective-permute-start | bytes 491528 | tf_op jit(solution)/shard_map/ppermute | solution.py:772
  80.0 16.9 %collective-permute-done.10.refs_7_ = f32[10,2,16,128]{3,2,1,0:T(8,128)S(1)} collective-permute-done((f32[10,2,16,128]{3,2,1,0:T(8,128)}, f32[10,2,16,128]{3,2,1,0:T(8,128)S(1)}, u32[]{:S(2)}, u32[]{:S(2)}) %collective-permute-start.10) | collective-permute-done | bytes 163872 | tf_op jit(solution)/shard_map/ppermute | solution.py:772
  98.5 2.0 collective-permute-done.11.refs_8_
  100.5 2.7 %collective-permute-start.17 = (f32[10,2,16,128]{3,2,1,0:T(8,128)}, f32[10,2,16,128]{3,2,1,0:T(8,128)S(1)}, u32[]{:S(2)}, u32[]{:S(2)}) collective-permute-start(f32[10,2,16,128]{3,2,1,0:T(8,128)} %get-tuple-element.41), channel_id=1, source_target_pairs={{0,3},{1,0},{2,1},{3,2},{4,7},{5,4},{6,5},{7,6},{8,11},{9,8},{10,9... | collective-permute-start | bytes 491528 | tf_op jit(solution)/shard_map/ppermute | solution.py:772
  103.1 4.1 %collective-permute-start.3 = (f32[10,2,16,128]{3,2,1,0:T(8,128)}, f32[10,2,16,128]{3,2,1,0:T(8,128)}, u32[]{:S(2)}, u32[]{:S(2)}) collective-permute-start(f32[10,2,16,128]{3,2,1,0:T(8,128)} %get-tuple-element.27), channel_id=1, source_target_pairs={{0,10},{1,11},{2,8},{3,9},{4,14},{5,15},{6,12},{7,13},{8,2},{9,3},... | collective-permute-start | bytes 491528 | tf_op jit(solution)/shard_map/ppermute | solution.py:772
  107.3 3.3 %collective-permute-start.5 = (f32[10,2,16,128]{3,2,1,0:T(8,128)}, f32[10,2,16,128]{3,2,1,0:T(8,128)}, u32[]{:S(2)}, u32[]{:S(2)}) collective-permute-start(f32[10,2,16,128]{3,2,1,0:T(8,128)} %get-tuple-element.29), channel_id=1, source_target_pairs={{0,6},{1,7},{2,4},{3,5},{4,10},{5,11},{6,8},{7,9},{8,14},{9,15},{1... | collective-permute-start | bytes 491528 | tf_op jit(solution)/shard_map/ppermute | solution.py:772
  112.4 4.3 %collective-permute-start.7 = (f32[10,2,16,128]{3,2,1,0:T(8,128)}, f32[10,2,16,128]{3,2,1,0:T(8,128)}, u32[]{:S(2)}, u32[]{:S(2)}) collective-permute-start(f32[10,2,16,128]{3,2,1,0:T(8,128)} %get-tuple-element.31), channel_id=1, source_target_pairs={{0,11},{1,8},{2,9},{3,10},{4,15},{5,12},{6,13},{7,14},{8,3},{9,0},... | collective-permute-start | bytes 491528 | tf_op jit(solution)/shard_map/ppermute | solution.py:772
  117.7 1.9 collective-permute-done.5.refs_2_
  119.6 2.9 %collective-permute-done.6.refs_3_ = f32[10,2,16,128]{3,2,1,0:T(8,128)} collective-permute-done((f32[10,2,16,128]{3,2,1,0:T(8,128)}, f32[10,2,16,128]{3,2,1,0:T(8,128)}, u32[]{:S(2)}, u32[]{:S(2)}) %collective-permute-start.6) | collective-permute-done | bytes 163872 | tf_op jit(solution)/shard_map/ppermute | solution.py:772
  122.5 2.5 %collective-permute-done.7.refs_4_ = f32[10,2,16,128]{3,2,1,0:T(8,128)} collective-permute-done((f32[10,2,16,128]{3,2,1,0:T(8,128)}, f32[10,2,16,128]{3,2,1,0:T(8,128)}, u32[]{:S(2)}, u32[]{:S(2)}) %collective-permute-start.7) | collective-permute-done | bytes 163872 | tf_op jit(solution)/shard_map/ppermute | solution.py:772
  125.0 9.8 %collective-permute-done.8.refs_5_ = f32[10,2,16,128]{3,2,1,0:T(8,128)} collective-permute-done((f32[10,2,16,128]{3,2,1,0:T(8,128)}, f32[10,2,16,128]{3,2,1,0:T(8,128)}, u32[]{:S(2)}, u32[]{:S(2)}) %collective-permute-start.8) | collective-permute-done | bytes 163872 | tf_op jit(solution)/shard_map/ppermute | solution.py:772
  134.9 9.2 %shard_map.164 = f32[128,2,16,128]{3,2,1,0:T(8,128)} custom-call(s32[1]{0:T(128)} %bitcast.8.me_ref, f32[10,2,16,128]{3,2,1,0:T(8,128)} %collective-permute-done.3.refs_0_, f32[10,2,16,128]{3,2,1,0:T(8,128)} %collective-permute-done.4.refs_1_, f32[10,2,16,128]{3,2,1,0:T(8,128)} %collective-permute-done.5.refs_2_, ...), custom_call_target="tpu_custom_call" | custom-call | flops 10000000000 | bytes 6000000 | tf_op jit(solution)/shard_map/pallas_call | solution.py:434
  144.1 5.8 %all-to-all-start.2 = ((f32[128,2,16,128]{3,2,1,0:T(8,128)}), f32[128,2,16,128]{3,2,1,0:T(8,128)}, u32[]{:S(2)}, u32[]{:S(2)}) async-start(f32[128,2,16,128]{3,2,1,0:T(8,128)} %shard_map.164), calls=%async_computation.2 | async-start | bytes 4194304 | tf_op jit(solution)/shard_map/all_to_all | solution.py:751
  150.4 7.6 %collective-permute-start = (s32[16]{0:T(128)S(1)}, s32[16]{0:T(128)S(1)}, u32[]{:S(2)}, u32[]{:S(2)}) collective-permute-start(s32[16]{0:T(128)S(1)} %pad_add_fusion), channel_id=1, source_target_pairs={{0,0},{1,16},{2,1},{3,17},{4,5},{5,21},{6,4},{7,20},{8,8},{9,24},{... | collective-permute-start | bytes 200 | tf_op jit(solution)/shard_map/ppermute | solution.py:736
  158.8 3.9 %prep.1.a_hbm = bf16[16,256,256]{2,1,0:T(8,128)(2,1)} custom-call(f32[2,16,128]{2,1,0:T(8,128)} %bitcast.26, f32[2,128,128]{2,1,0:T(8,128)} %constant.113.clone.dft_ref, f32[2,16,128]{2,1,0:T(8,128)} %constant.114.clone.turn_ref, f32[16,2,128]{2,1,0:T(2,128)} %constant.115.clone.wrap_ref), custom_call_target="tpu_custom_call" | custom-call | flops 2000000000 | bytes 5000000 | tf_op jit(solution)/shard_map/prep/pallas_call | solution.py:492
  162.7 5.4 %slave_azimuth.1 = (f32[2112,128]{1,0:T(8,128)S(1)}, f32[2112,128]{1,0:T(8,128)}) custom-call(f32[16,8,2,16,128]{4,3,2,1,0:T(8,128)S(1)} %bitcast.21, bf16[16,256,256]{2,1,0:T(8,128)(2,1)} %prep.1.a_hbm), custom_call_target="tpu_custom_call" | custom-call | flops 5000000000 | bytes 10000000 | tf_op jit(solution)/shard_map/slave_azimuth/pallas_call | solution.py:592
  170.1 2.5 %collective-permute-start.2 = (f32[2112,128]{1,0:T(8,128)S(1)}, f32[2112,128]{1,0:T(8,128)}, u32[]{:S(2)}, u32[]{:S(2)}) collective-permute-start(f32[2112,128]{1,0:T(8,128)S(1)} %get-tuple-element.26.refs_1_), channel_id=1, source_target_pairs={{16,0},{1,16},{17,1},{5,17},{21,5},{4,21},{20,4},{8,20},{24,8},{9,... | collective-permute-start | bytes 3244040 | tf_op jit(solution)/shard_map/ppermute | solution.py:742
  175.2 4.0 %all-to-all-done.2 = f32[128,2,16,128]{3,2,1,0:T(8,128)} async-done(((f32[128,2,16,128]{3,2,1,0:T(8,128)}), f32[128,2,16,128]{3,2,1,0:T(8,128)}, u32[]{:S(2)}, u32[]{:S(2)}) %all-to-all-start.2) | async-done | bytes 2097184 | tf_op jit(solution)/shard_map/all_to_all | solution.py:751
  179.2 5.8 %master_azimuth.1.refs_4_ = f32[2,2048,128]{2,1,0:T(8,128)} custom-call(f32[16,8,2,16,128]{4,3,2,1,0:T(8,128)} %bitcast.13.x_hbm, bf16[16,256,256]{2,1,0:T(8,128)(2,1)} %prep.1.a_hbm), custom_call_target="tpu_custom_call" | custom-call | flops 5000000000 | bytes 10000000 | tf_op jit(solution)/shard_map/master_azimuth/pallas_call | solution.py:623
  186.7 5.5 %looks.1 = (f32[16,512]{1,0:T(8,128)S(1)}, f32[8,512]{1,0:T(8,128)S(1)}) custom-call(s32[16]{0:T(128)S(1)} %collective-permute-done.shift_ref, f32[2112,128]{1,0:T(8,128)S(1)} %collective-permute-done.1.refs_0_, f32[2112,128]{1,0:T(8,128)S(1)} %get-tuple-element.26.refs_1_, f32[2112,128]{1,0:T(8,128)} %get-tuple-element.25.refs_2_, ...), custom_call_target="tpu_custom_call" | custom-call | flops 5000000000 | bytes 10000000 | tf_op jit(solution)/shard_map/looks/pallas_call | solution.py:697
  192.1 5.1 %collective-permute-start.19 = (f32[8,512]{1,0:T(8,128)S(1)}, f32[8,512]{1,0:T(8,128)S(1)}, u32[]{:S(2)}, u32[]{:S(2)}) collective-permute-start(f32[8,512]{1,0:T(8,128)S(1)} %get-tuple-element.44), channel_id=1, source_target_pairs={{0,1},{16,2},{1,3},{17,4},{5,5},{21,6},{4,7},{20,8},{8,9},{24,10},... | collective-permute-start | bytes 49160 | tf_op jit(solution)/shard_map/ppermute | solution.py:788
  197.2 1.9 collective-permute-start.20
  201.2 3.8 %collective-permute-done.20.right_ref = f32[8,512]{1,0:T(8,128)S(1)} collective-permute-done((f32[8,512]{1,0:T(8,128)S(1)}, f32[8,512]{1,0:T(8,128)S(1)}, u32[]{:S(2)}, u32[]{:S(2)}) %collective-permute-start.20) | collective-permute-done | bytes 16416 | tf_op jit(solution)/shard_map/ppermute | solution.py:789
  205.0 2.7 %collective-permute-done.18.box_ref = f32[16,512]{1,0:T(8,128)S(1)} collective-permute-done((f32[16,512]{1,0:T(8,128)S(1)}, f32[16,512]{1,0:T(8,128)S(1)}, u32[]{:S(2)}, u32[]{:S(2)}) %collective-permute-start.18) | collective-permute-done | bytes 32800 | tf_op jit(solution)/shard_map/ppermute | solution.py:787
  (78 shorter events, 16.7 us)
Async XLA Ops:
  3.2 47.7 %all-to-all-start = ((f32[16,10,2,16,128]{4,3,2,1,0:T(8,128)}), f32[16,10,2,16,128]{4,3,2,1,0:T(8,128)}, u32[]{:S(2)}, u32[]{:S(2)}) async-start(f32[16,10,2,16,128]{4,3,2,1,0:T(8,128)} %pre.1), calls=%async_computation | async-start | bytes 5242880 | tf_op jit(solution)/shard_map/all_to_all | solution.py:768
  59.2 84.9 %all-to-all-start.1 = ((f32[128,2,16,128]{3,2,1,0:T(8,128)}), f32[128,2,16,128]{3,2,1,0:T(8,128)S(1)}, u32[]{:S(2)}, u32[]{:S(2)}) async-start(f32[128,2,16,128]{3,2,1,0:T(8,128)} %shard_map.163), calls=%async_computation.1 | async-start | bytes 4194304 | tf_op jit(solution)/shard_map/all_to_all | solution.py:751
  70.5 26.5 %collective-permute-start.10 = (f32[10,2,16,128]{3,2,1,0:T(8,128)}, f32[10,2,16,128]{3,2,1,0:T(8,128)S(1)}, u32[]{:S(2)}, u32[]{:S(2)}) collective-permute-start(f32[10,2,16,128]{3,2,1,0:T(8,128)} %get-tuple-element.34), channel_id=1, source_target_pairs={{0,13},{1,14},{2,15},{3,12},{4,1},{5,2},{6,3},{7,0},{8,5},{9,6},{1... | collective-permute-start | bytes 491528 | tf_op jit(solution)/shard_map/ppermute | solution.py:772
  74.7 25.8 %collective-permute-start.11 = (f32[10,2,16,128]{3,2,1,0:T(8,128)}, f32[10,2,16,128]{3,2,1,0:T(8,128)S(1)}, u32[]{:S(2)}, u32[]{:S(2)}) collective-permute-start(f32[10,2,16,128]{3,2,1,0:T(8,128)} %get-tuple-element.35), channel_id=1, source_target_pairs={{0,2},{1,3},{2,0},{3,1},{4,6},{5,7},{6,4},{7,5},{8,10},{9,11},{10,... | collective-permute-start | bytes 491528 | tf_op jit(solution)/shard_map/ppermute | solution.py:772
  77.1 23.3 %collective-permute-start.12 = (f32[10,2,16,128]{3,2,1,0:T(8,128)}, f32[10,2,16,128]{3,2,1,0:T(8,128)S(1)}, u32[]{:S(2)}, u32[]{:S(2)}) collective-permute-start(f32[10,2,16,128]{3,2,1,0:T(8,128)} %get-tuple-element.36), channel_id=1, source_target_pairs={{0,7},{1,4},{2,5},{3,6},{4,11},{5,8},{6,9},{7,10},{8,15},{9,12},{1... | collective-permute-start | bytes 491528 | tf_op jit(solution)/shard_map/ppermute | solution.py:772
  77.1 26.0 %collective-permute-start.13 = (f32[10,2,16,128]{3,2,1,0:T(8,128)}, f32[10,2,16,128]{3,2,1,0:T(8,128)S(1)}, u32[]{:S(2)}, u32[]{:S(2)}) collective-permute-start(f32[10,2,16,128]{3,2,1,0:T(8,128)} %get-tuple-element.37), channel_id=1, source_target_pairs={{0,15},{1,12},{2,13},{3,14},{4,3},{5,0},{6,1},{7,2},{8,7},{9,4},{1... | collective-permute-start | bytes 491528 | tf_op jit(solution)/shard_map/ppermute | solution.py:772
  80.0 27.2 %collective-permute-start.14 = (f32[10,2,16,128]{3,2,1,0:T(8,128)}, f32[10,2,16,128]{3,2,1,0:T(8,128)S(1)}, u32[]{:S(2)}, u32[]{:S(2)}) collective-permute-start(f32[10,2,16,128]{3,2,1,0:T(8,128)} %get-tuple-element.38), channel_id=1, source_target_pairs={{0,4},{1,5},{2,6},{3,7},{4,8},{5,9},{6,10},{7,11},{8,12},{9,13},{1... | collective-permute-start | bytes 491528 | tf_op jit(solution)/shard_map/ppermute | solution.py:772
  96.9 37.9 %copy-start.6 = (f32[10,2,16,128]{3,2,1,0:T(8,128)}, f32[10,2,16,128]{3,2,1,0:T(8,128)S(1)}, u32[]{:S(2)}) copy-start(f32[10,2,16,128]{3,2,1,0:T(8,128)S(1)} %collective-permute-done.10.refs_7_) | copy-start | bytes 491524
  96.9 10.3 %collective-permute-start.15 = (f32[10,2,16,128]{3,2,1,0:T(8,128)}, f32[10,2,16,128]{3,2,1,0:T(8,128)S(1)}, u32[]{:S(2)}, u32[]{:S(2)}) collective-permute-start(f32[10,2,16,128]{3,2,1,0:T(8,128)} %get-tuple-element.39), channel_id=1, source_target_pairs={{0,12},{1,13},{2,14},{3,15},{4,0},{5,1},{6,2},{7,3},{8,4},{9,5},{1... | collective-permute-start | bytes 491528 | tf_op jit(solution)/shard_map/ppermute | solution.py:772
  100.4 34.4 %copy-start.7 = (f32[10,2,16,128]{3,2,1,0:T(8,128)}, f32[10,2,16,128]{3,2,1,0:T(8,128)S(1)}, u32[]{:S(2)}) copy-start(f32[10,2,16,128]{3,2,1,0:T(8,128)S(1)} %collective-permute-done.11.refs_8_) | copy-start | bytes 491524
  100.4 10.1 %collective-permute-start.16 = (f32[10,2,16,128]{3,2,1,0:T(8,128)}, f32[10,2,16,128]{3,2,1,0:T(8,128)S(1)}, u32[]{:S(2)}, u32[]{:S(2)}) collective-permute-start(f32[10,2,16,128]{3,2,1,0:T(8,128)} %get-tuple-element.40), channel_id=1, source_target_pairs={{0,1},{1,2},{2,3},{3,0},{4,5},{5,6},{6,7},{7,4},{8,9},{9,10},{10,1... | collective-permute-start | bytes 491528 | tf_op jit(solution)/shard_map/ppermute | solution.py:772
  100.5 34.4 %copy-start.8 = (f32[10,2,16,128]{3,2,1,0:T(8,128)}, f32[10,2,16,128]{3,2,1,0:T(8,128)S(1)}, u32[]{:S(2)}) copy-start(f32[10,2,16,128]{3,2,1,0:T(8,128)S(1)} %collective-permute-done.12.refs_9_) | copy-start | bytes 491524
  100.5 12.0 %collective-permute-start.17 = (f32[10,2,16,128]{3,2,1,0:T(8,128)}, f32[10,2,16,128]{3,2,1,0:T(8,128)S(1)}, u32[]{:S(2)}, u32[]{:S(2)}) collective-permute-start(f32[10,2,16,128]{3,2,1,0:T(8,128)} %get-tuple-element.41), channel_id=1, source_target_pairs={{0,3},{1,0},{2,1},{3,2},{4,7},{5,4},{6,5},{7,6},{8,11},{9,8},{10,9... | collective-permute-start | bytes 491528 | tf_op jit(solution)/shard_map/ppermute | solution.py:772
  103.1 31.7 %copy-start.9 = (f32[10,2,16,128]{3,2,1,0:T(8,128)}, f32[10,2,16,128]{3,2,1,0:T(8,128)S(1)}, u32[]{:S(2)}) copy-start(f32[10,2,16,128]{3,2,1,0:T(8,128)S(1)} %collective-permute-done.13.refs_10_) | copy-start | bytes 491524
  103.1 13.6 %collective-permute-start.3 = (f32[10,2,16,128]{3,2,1,0:T(8,128)}, f32[10,2,16,128]{3,2,1,0:T(8,128)}, u32[]{:S(2)}, u32[]{:S(2)}) collective-permute-start(f32[10,2,16,128]{3,2,1,0:T(8,128)} %get-tuple-element.27), channel_id=1, source_target_pairs={{0,10},{1,11},{2,8},{3,9},{4,14},{5,15},{6,12},{7,13},{8,2},{9,3},... | collective-permute-start | bytes 491528 | tf_op jit(solution)/shard_map/ppermute | solution.py:772
  107.2 27.6 %copy-start.10 = (f32[10,2,16,128]{3,2,1,0:T(8,128)}, f32[10,2,16,128]{3,2,1,0:T(8,128)S(1)}, u32[]{:S(2)}) copy-start(f32[10,2,16,128]{3,2,1,0:T(8,128)S(1)} %collective-permute-done.14.refs_11_) | copy-start | bytes 491524
  107.2 10.5 %collective-permute-start.4 = (f32[10,2,16,128]{3,2,1,0:T(8,128)}, f32[10,2,16,128]{3,2,1,0:T(8,128)}, u32[]{:S(2)}, u32[]{:S(2)}) collective-permute-start(f32[10,2,16,128]{3,2,1,0:T(8,128)} %get-tuple-element.28), channel_id=1, source_target_pairs={{0,9},{1,10},{2,11},{3,8},{4,13},{5,14},{6,15},{7,12},{8,1},{9,2},... | collective-permute-start | bytes 491528 | tf_op jit(solution)/shard_map/ppermute | solution.py:772
  107.2 27.6 %copy-start.11 = (f32[10,2,16,128]{3,2,1,0:T(8,128)}, f32[10,2,16,128]{3,2,1,0:T(8,128)S(1)}, u32[]{:S(2)}) copy-start(f32[10,2,16,128]{3,2,1,0:T(8,128)S(1)} %collective-permute-done.15.refs_12_) | copy-start | bytes 491524
  107.3 12.4 %collective-permute-start.5 = (f32[10,2,16,128]{3,2,1,0:T(8,128)}, f32[10,2,16,128]{3,2,1,0:T(8,128)}, u32[]{:S(2)}, u32[]{:S(2)}) collective-permute-start(f32[10,2,16,128]{3,2,1,0:T(8,128)} %get-tuple-element.29), channel_id=1, source_target_pairs={{0,6},{1,7},{2,4},{3,5},{4,10},{5,11},{6,8},{7,9},{8,14},{9,15},{1... | collective-permute-start | bytes 491528 | tf_op jit(solution)/shard_map/ppermute | solution.py:772
  110.6 24.3 %copy-start.12 = (f32[10,2,16,128]{3,2,1,0:T(8,128)}, f32[10,2,16,128]{3,2,1,0:T(8,128)S(1)}, u32[]{:S(2)}) copy-start(f32[10,2,16,128]{3,2,1,0:T(8,128)S(1)} %collective-permute-done.16.refs_13_) | copy-start | bytes 491524
  110.6 12.0 %collective-permute-start.6 = (f32[10,2,16,128]{3,2,1,0:T(8,128)}, f32[10,2,16,128]{3,2,1,0:T(8,128)}, u32[]{:S(2)}, u32[]{:S(2)}) collective-permute-start(f32[10,2,16,128]{3,2,1,0:T(8,128)} %get-tuple-element.30), channel_id=1, source_target_pairs={{0,14},{1,15},{2,12},{3,13},{4,2},{5,3},{6,0},{7,1},{8,6},{9,7},{1... | collective-permute-start | bytes 491528 | tf_op jit(solution)/shard_map/ppermute | solution.py:772
  112.4 22.5 %copy-start.13 = (f32[10,2,16,128]{3,2,1,0:T(8,128)}, f32[10,2,16,128]{3,2,1,0:T(8,128)S(1)}, u32[]{:S(2)}) copy-start(f32[10,2,16,128]{3,2,1,0:T(8,128)S(1)} %collective-permute-done.17.refs_14_) | copy-start | bytes 491524
  112.4 12.6 %collective-permute-start.7 = (f32[10,2,16,128]{3,2,1,0:T(8,128)}, f32[10,2,16,128]{3,2,1,0:T(8,128)}, u32[]{:S(2)}, u32[]{:S(2)}) collective-permute-start(f32[10,2,16,128]{3,2,1,0:T(8,128)} %get-tuple-element.31), channel_id=1, source_target_pairs={{0,11},{1,8},{2,9},{3,10},{4,15},{5,12},{6,13},{7,14},{8,3},{9,0},... | collective-permute-start | bytes 491528 | tf_op jit(solution)/shard_map/ppermute | solution.py:772
  116.7 18.1 %collective-permute-start.8 = (f32[10,2,16,128]{3,2,1,0:T(8,128)}, f32[10,2,16,128]{3,2,1,0:T(8,128)}, u32[]{:S(2)}, u32[]{:S(2)}) collective-permute-start(f32[10,2,16,128]{3,2,1,0:T(8,128)} %get-tuple-element.32), channel_id=1, source_target_pairs={{0,8},{1,9},{2,10},{3,11},{4,12},{5,13},{6,14},{7,15},{8,0},{9,1},... | collective-permute-start | bytes 491528 | tf_op jit(solution)/shard_map/ppermute | solution.py:772
  117.7 17.1 %collective-permute-start.9 = (f32[10,2,16,128]{3,2,1,0:T(8,128)}, f32[10,2,16,128]{3,2,1,0:T(8,128)}, u32[]{:S(2)}, u32[]{:S(2)}) collective-permute-start(f32[10,2,16,128]{3,2,1,0:T(8,128)} %get-tuple-element.33), channel_id=1, source_target_pairs={{0,5},{1,6},{2,7},{3,4},{4,9},{5,10},{6,11},{7,8},{8,13},{9,14},{1... | collective-permute-start | bytes 491528 | tf_op jit(solution)/shard_map/ppermute | solution.py:772
  144.1 35.1 %all-to-all-start.2 = ((f32[128,2,16,128]{3,2,1,0:T(8,128)}), f32[128,2,16,128]{3,2,1,0:T(8,128)}, u32[]{:S(2)}, u32[]{:S(2)}) async-start(f32[128,2,16,128]{3,2,1,0:T(8,128)} %shard_map.164), calls=%async_computation.2 | async-start | bytes 4194304 | tf_op jit(solution)/shard_map/all_to_all | solution.py:751
  150.4 34.6 %collective-permute-start = (s32[16]{0:T(128)S(1)}, s32[16]{0:T(128)S(1)}, u32[]{:S(2)}, u32[]{:S(2)}) collective-permute-start(s32[16]{0:T(128)S(1)} %pad_add_fusion), channel_id=1, source_target_pairs={{0,0},{1,16},{2,1},{3,17},{4,5},{5,21},{6,4},{7,20},{8,8},{9,24},{... | collective-permute-start | bytes 200 | tf_op jit(solution)/shard_map/ppermute | solution.py:736
  168.2 16.8 %collective-permute-start.1 = (f32[2112,128]{1,0:T(8,128)}, f32[2112,128]{1,0:T(8,128)S(1)}, u32[]{:S(2)}, u32[]{:S(2)}) collective-permute-start(f32[2112,128]{1,0:T(8,128)} %get-tuple-element.25.refs_2_), channel_id=1, source_target_pairs={{0,16},{16,1},{1,17},{17,5},{5,21},{21,4},{4,20},{20,8},{8,24},{24... | collective-permute-start | bytes 3244040 | tf_op jit(solution)/shard_map/ppermute | solution.py:742
  170.1 16.6 %collective-permute-start.2 = (f32[2112,128]{1,0:T(8,128)S(1)}, f32[2112,128]{1,0:T(8,128)}, u32[]{:S(2)}, u32[]{:S(2)}) collective-permute-start(f32[2112,128]{1,0:T(8,128)S(1)} %get-tuple-element.26.refs_1_), channel_id=1, source_target_pairs={{16,0},{1,16},{17,1},{5,17},{21,5},{4,21},{20,4},{8,20},{24,8},{9,... | collective-permute-start | bytes 3244040 | tf_op jit(solution)/shard_map/ppermute | solution.py:742
  192.1 9.1 %collective-permute-start.19 = (f32[8,512]{1,0:T(8,128)S(1)}, f32[8,512]{1,0:T(8,128)S(1)}, u32[]{:S(2)}, u32[]{:S(2)}) collective-permute-start(f32[8,512]{1,0:T(8,128)S(1)} %get-tuple-element.44), channel_id=1, source_target_pairs={{0,1},{16,2},{1,3},{17,4},{5,5},{21,6},{4,7},{20,8},{8,9},{24,10},... | collective-permute-start | bytes 49160 | tf_op jit(solution)/shard_map/ppermute | solution.py:788
  197.2 7.8 %collective-permute-start.20 = (f32[8,512]{1,0:T(8,128)S(1)}, f32[8,512]{1,0:T(8,128)S(1)}, u32[]{:S(2)}, u32[]{:S(2)}) collective-permute-start(f32[8,512]{1,0:T(8,128)S(1)} %get-tuple-element.44), channel_id=1, source_target_pairs={{16,0},{1,1},{17,2},{5,3},{21,4},{4,5},{20,6},{8,7},{24,8},{9,9},{... | collective-permute-start | bytes 49160 | tf_op jit(solution)/shard_map/ppermute | solution.py:789
  199.2 8.6 %collective-permute-start.18 = (f32[16,512]{1,0:T(8,128)S(1)}, f32[16,512]{1,0:T(8,128)S(1)}, u32[]{:S(2)}, u32[]{:S(2)}) collective-permute-start(f32[16,512]{1,0:T(8,128)S(1)} %get-tuple-element.43), channel_id=1, source_target_pairs={{0,0},{16,1},{1,2},{17,3},{5,4},{21,5},{4,6},{20,7},{8,8},{24,9},{... | collective-permute-start | bytes 98312 | tf_op jit(solution)/shard_map/ppermute | solution.py:787
  (6 other events, 51.7 us)

commit v2 on v1

--- a/solution.py
+++ b/solution.py
@@ -27,7 +27,7 @@
 
 SHIFTS = sorted(
     ((dx, dz) for dx in range(4) for dz in range(4)),
-    key=lambda s: -(min(s[0], 4 - s[0]) + min(s[1], 4 - s[1])),
+    key=lambda s: min(s[0], 4 - s[0]) + min(s[1], 4 - s[1]),
 )
 
 
@@ -713,23 +713,41 @@
     )(shifts, *packs, master, counts, TABLES["pick"])
 
 
-def _final_kernel(box_ref, left_ref, right_ref, scale_ref, o_ref):
+def _merge_kernel(core_ref, box_ref, side_ref, o_ref):
+    row = lax.broadcasted_iota(jnp.int32, (16, 512), 0)
+    first = core_ref[0] == 0
+    facing = jnp.where(first, side_ref[0:1, :], side_ref[1:2, :])
+    o_ref[...] = box_ref[...] + jnp.where(row == jnp.where(first, 15, 0), facing, 0.0)
+
+
+def merge(core, box, side):
+    return pl.pallas_call(
+        _merge_kernel,
+        in_specs=[SMEM, VMEM, VMEM],
+        out_shape=jax.ShapeDtypeStruct((16, 512), F32),
+        compiler_params=limit(4),
+        name="merge",
+    )(core, box, side)
+
+
+def _final_kernel(odd_ref, box_ref, outer_ref, scale_ref, o_ref):
     row = lax.broadcasted_iota(jnp.int32, (16, 256), 0)
+    odd = odd_ref[0] == 1
+    at = jnp.where(odd, 15, 0)
     for c in range(2):
-        at = slice(256 * c, 256 * c + 256)
-        x = box_ref[:, at]
-        x = x + jnp.where(row == 0, left_ref[1:2, at], 0.0)
-        x = x + jnp.where(row == 15, right_ref[0:1, at], 0.0)
-        o_ref[c] = x * scale_ref[...]
-
-
-def final(box, left, right, scale):
+        cells = slice(256 * c, 256 * c + 256)
+        outer = jnp.where(odd, outer_ref[0:1, cells], outer_ref[1:2, cells])
+        o_ref[c] = (box_ref[:, cells] + jnp.where(row == at, outer, 0.0)) * scale_ref[...]
+
+
+def final(odd, box, outer, scale):
     return pl.pallas_call(
         _final_kernel,
+        in_specs=[SMEM, VMEM, VMEM, VMEM],
         out_shape=jax.ShapeDtypeStruct((2, 16, 256), F32),
         compiler_params=limit(4),
         name="final",
-    )(box, left, right, scale)
+    )(odd, box, outer, scale)
 
 
 def to_worker(x):
@@ -784,10 +802,18 @@
     master = master_azimuth(master, matrices)
     box, side = looks(shifts, (from_left, low, high, from_right), master, col_counts)
 
+    core = (lax.axis_index("az") % 2).astype(jnp.int32)[None]
+    odd = (lax.axis_index("rg") % 2).astype(jnp.int32)[None]
+    facing = lax.ppermute(side, ALL, [(worker(b), worker(b ^ 1)) for b in range(128)])
+    outer = lax.ppermute(
+        side,
+        ALL,
+        [(worker(b - 1), b) for b in range(2, 128, 2)]
+        + [(worker(b + 1), b) for b in range(1, 126, 2)],
+    )
+    box = merge(core, box, facing)
     box = lax.ppermute(box, ALL, [(worker(b), b) for b in range(128)])
-    left = lax.ppermute(side, ALL, [(worker(b), b + 1) for b in range(127)])
-    right = lax.ppermute(side, ALL, [(worker(b + 1), b) for b in range(127)])
-    return final(box, left, right, scale).transpose(0, 2, 1)
+    return final(odd, box, outer, scale).transpose(0, 2, 1)
 
 
 def solution(mesh):

time: 209 us -> 210 us (level)
  starting transfers between devices: 70.9 us -> 81 us
  waiting for transfers between devices: 85.2 us -> 75.6 us
    ppermute x15, waiting for transfers between devices: 36.2 us -> 30.4 us  [local(): lax.ppermute(piece, 'rg', [(r, shifted(r, shift)) for r in range(NP)])]
    all_to_all x2, starting transfers between devices: 13.3 us -> 18.4 us  [columns_of(): return lax.all_to_all(ranged, ALL, 0, 0, tiled=True)]
    ppermute x1, waiting for transfers between devices: 2.68 us -> 6.5 us  [local(): box = lax.ppermute(box, ALL, [(worker(b), b) for b in range(128)])]
    ppermute x2, waiting for transfers between devices: 3.84 us -> 0.01 us  [the longest x1 0.01 us: local(): lax.ppermute(side, ALL, [(worker(b - 1), b) for b in range(2, 128, 2)] +...]
    ppermute x15, starting transfers between devices: 28.1 us -> 31.5 us  [local(): lax.ppermute(piece, 'rg', [(r, shifted(r, shift)) for r in range(NP)])]
    all_to_all x2, waiting for transfers between devices: 3.99 us -> 1.56 us  [columns_of(): return lax.all_to_all(ranged, ALL, 0, 0, tiled=True)]
  transfers between devices with their start and end apart: 24 -> 24, of which waited for: 12 -> 11; matrix products, arithmetic and copies ran while one was open for 3% -> 3% of each run, Pallas kernels for 13% -> 13%
where the time goes in v2:
time: 210 us; the launch traced here: 209 us
  starting transfers between devices  81 us (39%)
  waiting for transfers between devices  75.6 us (36%)
  Pallas kernels  45.7 us (22%)
  local copies, waits for them, and re-layouts  4.6 us (2%)
    all_to_all x1, waiting for transfers between devices, local(): slave = lax.all_to_all(slave, 'rg', 0, 0, tiled=True)  36.8 us
    ppermute x15, starting transfers between devices, local(): lax.ppermute(piece, 'rg', [(r, shifted(r, shift)) for r in range(NP)])  31.5 us
    ppermute x15, waiting for transfers between devices, local(): lax.ppermute(piece, 'rg', [(r, shifted(r, shift)) for r in range(NP)])  30.4 us
    all_to_all x2, starting transfers between devices, columns_of(): return lax.all_to_all(ranged, ALL, 0, 0, tiled=True)  18.4 us
    pallas_call x2, Pallas kernels, range_compress(): pl.pallas_call(kernel, in_specs=specs + [HBM] * 7, out_specs=HBM, out_sha...  17.5 us
    ppermute x1, starting transfers between devices, to_worker(): return lax.ppermute(x, ALL, [(b, worker(b)) for b in range(128)])  8.87 us
    all_to_all x1, starting transfers between devices, local(): slave = lax.all_to_all(slave, 'rg', 0, 0, tiled=True)  8.6 us
    ppermute x1, waiting for transfers between devices, local(): box = lax.ppermute(box, ALL, [(worker(b), b) for b in range(128)])  6.5 us
  transfers between devices with their start and end apart: 24, of which 11 were waited for; matrix products, arithmetic and copies ran while one was open for 3% of the time, Pallas kernels for 13%

profile of v2, /device:TPU:1, one launch (start us, length us, event | category | flops | bytes accessed | tf_op | source)
XLA Modules:
  0.0 209.0 jit_solution(8417845466271852104)
XLA Ops:
  0.0 3.1 %pre.1 = f32[16,10,2,16,128]{4,3,2,1,0:T(8,128)} custom-call(f32[5000,128]{1,0:T(8,128)} %bitcast.25), custom_call_target="tpu_custom_call" | custom-call | flops 100000000 | bytes 10000000 | tf_op jit(solution)/shard_map/pre/pallas_call | solution.py:268
  3.2 8.6 %all-to-all-start = ((f32[16,10,2,16,128]{4,3,2,1,0:T(8,128)}), f32[16,10,2,16,128]{4,3,2,1,0:T(8,128)}, u32[]{:S(2)}, u32[]{:S(2)}) async-start(f32[16,10,2,16,128]{4,3,2,1,0:T(8,128)} %pre.1), calls=%async_computation | async-start | bytes 5242880 | tf_op jit(solution)/shard_map/all_to_all | solution.py:786
  14.1 36.8 %all-to-all-done.x_hbm = f32[16,10,2,16,128]{4,3,2,1,0:T(8,128)} async-done(((f32[16,10,2,16,128]{4,3,2,1,0:T(8,128)}), f32[16,10,2,16,128]{4,3,2,1,0:T(8,128)}, u32[]{:S(2)}, u32[]{:S(2)}) %all-to-all-start) | async-done | bytes 2621472 | tf_op jit(solution)/shard_map/all_to_all | solution.py:786
  50.9 8.3 %shard_map.163 = f32[128,2,16,128]{3,2,1,0:T(8,128)} custom-call(f32[16,10,2,16,128]{4,3,2,1,0:T(8,128)} %all-to-all-done.x_hbm, f32[10,2,128]{2,1,0:T(2,128)} %constant.113.clone.refs_0_.refs_16_, f32[160,2,128]{2,1,0:T(2,128)} %pad.8.refs_1_.refs_17_, bf16[256,256]{1,0:T(8,128)(2,1)} %constant.114.clone.refs_2_.refs_18_, ...), custom_call_target="tpu_custom_call" | custom-call | flops 10000000000 | bytes 6000000 | tf_op jit(solution)/shard_map/pallas_call | solution.py:434
  59.2 7.5 %all-to-all-start.1 = ((f32[128,2,16,128]{3,2,1,0:T(8,128)}), f32[128,2,16,128]{3,2,1,0:T(8,128)S(1)}, u32[]{:S(2)}, u32[]{:S(2)}) async-start(f32[128,2,16,128]{3,2,1,0:T(8,128)} %shard_map.163), calls=%async_computation.1 | async-start | bytes 4194304 | tf_op jit(solution)/shard_map/all_to_all | solution.py:769
  66.7 3.8 %pre_shifts.1 = (f32[10,2,16,128]{3,2,1,0:T(8,128)}, f32[10,2,16,128]{3,2,1,0:T(8,128)}, f32[10,2,16,128]{3,2,1,0:T(8,128)}, f32[10,2,16,128]{3,2,1,0:T(8,128)},...) custom-call(s32[1]{0:T(128)} %bitcast.10.me_ref, ...), custom_call_target="tpu_custom_call" | custom-call | flops 100000000 | bytes 10000000 | tf_op jit(solution)/shard_map/pre_shifts/pallas_call | solution.py:280
  70.5 2.9 %collective-permute-start.10 = (f32[10,2,16,128]{3,2,1,0:T(8,128)}, f32[10,2,16,128]{3,2,1,0:T(8,128)S(1)}, u32[]{:S(2)}, u32[]{:S(2)}) collective-permute-start(f32[10,2,16,128]{3,2,1,0:T(8,128)} %get-tuple-element.35), channel_id=1, source_target_pairs={{0,2},{1,3},{2,0},{3,1},{4,6},{5,7},{6,4},{7,5},{8,10},{9,11},{10,... | collective-permute-start | bytes 491528 | tf_op jit(solution)/shard_map/ppermute | solution.py:790
  73.4 1.9 collective-permute-start.11
  77.1 2.4 %collective-permute-start.13 = (f32[10,2,16,128]{3,2,1,0:T(8,128)}, f32[10,2,16,128]{3,2,1,0:T(8,128)S(1)}, u32[]{:S(2)}, u32[]{:S(2)}) collective-permute-start(f32[10,2,16,128]{3,2,1,0:T(8,128)} %get-tuple-element.38), channel_id=1, source_target_pairs={{0,9},{1,10},{2,11},{3,8},{4,13},{5,14},{6,15},{7,12},{8,1},{9,2},... | collective-permute-start | bytes 491528 | tf_op jit(solution)/shard_map/ppermute | solution.py:790
  81.0 14.6 %collective-permute-done.10.refs_8_ = f32[10,2,16,128]{3,2,1,0:T(8,128)S(1)} collective-permute-done((f32[10,2,16,128]{3,2,1,0:T(8,128)}, f32[10,2,16,128]{3,2,1,0:T(8,128)S(1)}, u32[]{:S(2)}, u32[]{:S(2)}) %collective-permute-start.10) | collective-permute-done | bytes 163872 | tf_op jit(solution)/shard_map/ppermute | solution.py:790
  95.6 3.1 %collective-permute-start.15 = (f32[10,2,16,128]{3,2,1,0:T(8,128)}, f32[10,2,16,128]{3,2,1,0:T(8,128)S(1)}, u32[]{:S(2)}, u32[]{:S(2)}) collective-permute-start(f32[10,2,16,128]{3,2,1,0:T(8,128)} %get-tuple-element.40), channel_id=1, source_target_pairs={{0,14},{1,15},{2,12},{3,13},{4,2},{5,3},{6,0},{7,1},{8,6},{9,7},{1... | collective-permute-start | bytes 491528 | tf_op jit(solution)/shard_map/ppermute | solution.py:790
  98.6 2.5 %collective-permute-done.11.refs_9_ = f32[10,2,16,128]{3,2,1,0:T(8,128)S(1)} collective-permute-done((f32[10,2,16,128]{3,2,1,0:T(8,128)}, f32[10,2,16,128]{3,2,1,0:T(8,128)S(1)}, u32[]{:S(2)}, u32[]{:S(2)}) %collective-permute-start.11) | collective-permute-done | bytes 163872 | tf_op jit(solution)/shard_map/ppermute | solution.py:790
  103.3 5.6 %collective-permute-start.17 = (f32[10,2,16,128]{3,2,1,0:T(8,128)}, f32[10,2,16,128]{3,2,1,0:T(8,128)S(1)}, u32[]{:S(2)}, u32[]{:S(2)}) collective-permute-start(f32[10,2,16,128]{3,2,1,0:T(8,128)} %get-tuple-element.42), channel_id=1, source_target_pairs={{0,10},{1,11},{2,8},{3,9},{4,14},{5,15},{6,12},{7,13},{8,2},{9,3},... | collective-permute-start | bytes 491528 | tf_op jit(solution)/shard_map/ppermute | solution.py:790
  109.1 2.5 %collective-permute-start.4 = (f32[10,2,16,128]{3,2,1,0:T(8,128)}, f32[10,2,16,128]{3,2,1,0:T(8,128)}, u32[]{:S(2)}, u32[]{:S(2)}) collective-permute-start(f32[10,2,16,128]{3,2,1,0:T(8,128)} %get-tuple-element.29), channel_id=1, source_target_pairs={{0,12},{1,13},{2,14},{3,15},{4,0},{5,1},{6,2},{7,3},{8,4},{9,5},{1... | collective-permute-start | bytes 491528 | tf_op jit(solution)/shard_map/ppermute | solution.py:790
  112.5 5.0 %collective-permute-done.16.refs_14_ = f32[10,2,16,128]{3,2,1,0:T(8,128)S(1)} collective-permute-done((f32[10,2,16,128]{3,2,1,0:T(8,128)}, f32[10,2,16,128]{3,2,1,0:T(8,128)S(1)}, u32[]{:S(2)}, u32[]{:S(2)}) %collective-permute-start.16) | collective-permute-done | bytes 163872 | tf_op jit(solution)/shard_map/ppermute | solution.py:790
  119.4 2.1 %collective-permute-done.3.refs_1_ = f32[10,2,16,128]{3,2,1,0:T(8,128)} collective-permute-done((f32[10,2,16,128]{3,2,1,0:T(8,128)}, f32[10,2,16,128]{3,2,1,0:T(8,128)}, u32[]{:S(2)}, u32[]{:S(2)}) %collective-permute-start.3) | collective-permute-done | bytes 163872 | tf_op jit(solution)/shard_map/ppermute | solution.py:790
  121.6 2.8 %collective-permute-start.8 = (f32[10,2,16,128]{3,2,1,0:T(8,128)}, f32[10,2,16,128]{3,2,1,0:T(8,128)}, u32[]{:S(2)}, u32[]{:S(2)}) collective-permute-start(f32[10,2,16,128]{3,2,1,0:T(8,128)} %get-tuple-element.33), channel_id=1, source_target_pairs={{0,5},{1,6},{2,7},{3,4},{4,9},{5,10},{6,11},{7,8},{8,13},{9,14},{1... | collective-permute-start | bytes 491528 | tf_op jit(solution)/shard_map/ppermute | solution.py:790
  124.4 2.5 %collective-permute-start.9 = (f32[10,2,16,128]{3,2,1,0:T(8,128)}, f32[10,2,16,128]{3,2,1,0:T(8,128)}, u32[]{:S(2)}, u32[]{:S(2)}) collective-permute-start(f32[10,2,16,128]{3,2,1,0:T(8,128)} %get-tuple-element.34), channel_id=1, source_target_pairs={{0,13},{1,14},{2,15},{3,12},{4,1},{5,2},{6,3},{7,0},{8,5},{9,6},{1... | collective-permute-start | bytes 491528 | tf_op jit(solution)/shard_map/ppermute | solution.py:790
  126.9 3.1 %collective-permute-done.8.refs_6_ = f32[10,2,16,128]{3,2,1,0:T(8,128)} collective-permute-done((f32[10,2,16,128]{3,2,1,0:T(8,128)}, f32[10,2,16,128]{3,2,1,0:T(8,128)}, u32[]{:S(2)}, u32[]{:S(2)}) %collective-permute-start.8) | collective-permute-done | bytes 163872 | tf_op jit(solution)/shard_map/ppermute | solution.py:790
  129.9 2.5 %collective-permute-done.9.refs_7_ = f32[10,2,16,128]{3,2,1,0:T(8,128)} collective-permute-done((f32[10,2,16,128]{3,2,1,0:T(8,128)}, f32[10,2,16,128]{3,2,1,0:T(8,128)}, u32[]{:S(2)}, u32[]{:S(2)}) %collective-permute-start.9) | collective-permute-done | bytes 163872 | tf_op jit(solution)/shard_map/ppermute | solution.py:790
  132.5 9.2 %shard_map.164 = f32[128,2,16,128]{3,2,1,0:T(8,128)} custom-call(s32[1]{0:T(128)} %bitcast.10.me_ref, f32[10,2,16,128]{3,2,1,0:T(8,128)} %get-tuple-element.27.refs_0_, f32[10,2,16,128]{3,2,1,0:T(8,128)} %collective-permute-done.3.refs_1_, f32[10,2,16,128]{3,2,1,0:T(8,128)} %collective-permute-done.4.refs_2_, ...), custom_call_target="tpu_custom_call" | custom-call | flops 10000000000 | bytes 6000000 | tf_op jit(solution)/shard_map/pallas_call | solution.py:434
  141.8 10.9 %all-to-all-start.2 = ((f32[128,2,16,128]{3,2,1,0:T(8,128)}), f32[128,2,16,128]{3,2,1,0:T(8,128)}, u32[]{:S(2)}, u32[]{:S(2)}) async-start(f32[128,2,16,128]{3,2,1,0:T(8,128)} %shard_map.164), calls=%async_computation.2 | async-start | bytes 4194304 | tf_op jit(solution)/shard_map/all_to_all | solution.py:769
  153.9 3.9 %prep.1.a_hbm = bf16[16,256,256]{2,1,0:T(8,128)(2,1)} custom-call(f32[2,16,128]{2,1,0:T(8,128)} %bitcast.28, f32[2,128,128]{2,1,0:T(8,128)} %constant.119.clone.dft_ref, f32[2,16,128]{2,1,0:T(8,128)} %constant.120.clone.turn_ref, f32[16,2,128]{2,1,0:T(2,128)} %constant.121.clone.wrap_ref), custom_call_target="tpu_custom_call" | custom-call | flops 2000000000 | bytes 5000000 | tf_op jit(solution)/shard_map/prep/pallas_call | solution.py:492
  157.8 5.4 %slave_azimuth.1 = (f32[2112,128]{1,0:T(8,128)S(1)}, f32[2112,128]{1,0:T(8,128)}) custom-call(f32[16,8,2,16,128]{4,3,2,1,0:T(8,128)S(1)} %bitcast.23, bf16[16,256,256]{2,1,0:T(8,128)(2,1)} %prep.1.a_hbm), custom_call_target="tpu_custom_call" | custom-call | flops 5000000000 | bytes 10000000 | tf_op jit(solution)/shard_map/slave_azimuth/pallas_call | solution.py:592
  163.3 3.5 %collective-permute-start.1 = (f32[2112,128]{1,0:T(8,128)}, f32[2112,128]{1,0:T(8,128)S(1)}, u32[]{:S(2)}, u32[]{:S(2)}) collective-permute-start(f32[2112,128]{1,0:T(8,128)} %get-tuple-element.25.refs_2_), channel_id=1, source_target_pairs={{0,16},{16,1},{1,17},{17,5},{5,21},{21,4},{4,20},{20,8},{8,24},{24... | collective-permute-start | bytes 3244040 | tf_op jit(solution)/shard_map/ppermute | solution.py:760
  166.8 1.9 collective-permute-start.2
  168.8 8.9 %collective-permute-start = (s32[16]{0:T(128)S(1)}, s32[16]{0:T(128)S(1)}, u32[]{:S(2)}, u32[]{:S(2)}) collective-permute-start(s32[16]{0:T(128)S(1)} %pad_add_fusion), channel_id=1, source_target_pairs={{0,0},{1,16},{2,1},{3,17},{4,5},{5,21},{6,4},{7,20},{8,8},{9,24},{... | collective-permute-start | bytes 200 | tf_op jit(solution)/shard_map/ppermute | solution.py:754
  181.9 5.8 %master_azimuth.1.refs_4_ = f32[2,2048,128]{2,1,0:T(8,128)} custom-call(f32[16,8,2,16,128]{4,3,2,1,0:T(8,128)} %bitcast.15.x_hbm, bf16[16,256,256]{2,1,0:T(8,128)(2,1)} %prep.1.a_hbm), custom_call_target="tpu_custom_call" | custom-call | flops 5000000000 | bytes 10000000 | tf_op jit(solution)/shard_map/master_azimuth/pallas_call | solution.py:623
  188.1 5.5 %looks.1 = (f32[16,512]{1,0:T(8,128)S(1)}, f32[8,512]{1,0:T(8,128)S(1)}) custom-call(s32[16]{0:T(128)S(1)} %collective-permute-done.shift_ref, f32[2112,128]{1,0:T(8,128)S(1)} %collective-permute-done.1.refs_0_, f32[2112,128]{1,0:T(8,128)S(1)} %get-tuple-element.26.refs_1_, f32[2112,128]{1,0:T(8,128)} %get-tuple-element.25.refs_2_, ...), custom_call_target="tpu_custom_call" | custom-call | flops 5000000000 | bytes 10000000 | tf_op jit(solution)/shard_map/looks/pallas_call | solution.py:697
  194.7 5.1 %collective-permute-start.20 = (f32[8,512]{1,0:T(8,128)S(1)}, f32[8,512]{1,0:T(8,128)S(1)}, u32[]{:S(2)}, u32[]{:S(2)}) collective-permute-start(f32[8,512]{1,0:T(8,128)S(1)} %get-tuple-element.44), channel_id=1, source_target_pairs={{16,2},{17,4},{21,6},{20,8},{24,10},{25,12},{29,14},{28,16},{31,18... | collective-permute-start | bytes 49160 | tf_op jit(solution)/shard_map/ppermute | solution.py:808
  199.8 1.9 collective-permute-start.19
  201.9 6.5 %collective-permute-done.19.box_ref = f32[16,512]{1,0:T(8,128)S(1)} collective-permute-done((f32[16,512]{1,0:T(8,128)S(1)}, f32[16,512]{1,0:T(8,128)S(1)}, u32[]{:S(2)}, u32[]{:S(2)}) %collective-permute-start.19) | collective-permute-done | bytes 32800 | tf_op jit(solution)/shard_map/ppermute | solution.py:815
  (79 shorter events, 18.3 us)
Async XLA Ops:
  3.2 47.7 %all-to-all-start = ((f32[16,10,2,16,128]{4,3,2,1,0:T(8,128)}), f32[16,10,2,16,128]{4,3,2,1,0:T(8,128)}, u32[]{:S(2)}, u32[]{:S(2)}) async-start(f32[16,10,2,16,128]{4,3,2,1,0:T(8,128)} %pre.1), calls=%async_computation | async-start | bytes 5242880 | tf_op jit(solution)/shard_map/all_to_all | solution.py:786
  59.2 82.5 %all-to-all-start.1 = ((f32[128,2,16,128]{3,2,1,0:T(8,128)}), f32[128,2,16,128]{3,2,1,0:T(8,128)S(1)}, u32[]{:S(2)}, u32[]{:S(2)}) async-start(f32[128,2,16,128]{3,2,1,0:T(8,128)} %shard_map.163), calls=%async_computation.1 | async-start | bytes 4194304 | tf_op jit(solution)/shard_map/all_to_all | solution.py:769
  70.5 25.1 %collective-permute-start.10 = (f32[10,2,16,128]{3,2,1,0:T(8,128)}, f32[10,2,16,128]{3,2,1,0:T(8,128)S(1)}, u32[]{:S(2)}, u32[]{:S(2)}) collective-permute-start(f32[10,2,16,128]{3,2,1,0:T(8,128)} %get-tuple-element.35), channel_id=1, source_target_pairs={{0,2},{1,3},{2,0},{3,1},{4,6},{5,7},{6,4},{7,5},{8,10},{9,11},{10,... | collective-permute-start | bytes 491528 | tf_op jit(solution)/shard_map/ppermute | solution.py:790
  73.4 27.7 %collective-permute-start.11 = (f32[10,2,16,128]{3,2,1,0:T(8,128)}, f32[10,2,16,128]{3,2,1,0:T(8,128)S(1)}, u32[]{:S(2)}, u32[]{:S(2)}) collective-permute-start(f32[10,2,16,128]{3,2,1,0:T(8,128)} %get-tuple-element.36), channel_id=1, source_target_pairs={{0,7},{1,4},{2,5},{3,6},{4,11},{5,8},{6,9},{7,10},{8,15},{9,12},{1... | collective-permute-start | bytes 491528 | tf_op jit(solution)/shard_map/ppermute | solution.py:790
  75.4 28.0 %collective-permute-start.12 = (f32[10,2,16,128]{3,2,1,0:T(8,128)}, f32[10,2,16,128]{3,2,1,0:T(8,128)S(1)}, u32[]{:S(2)}, u32[]{:S(2)}) collective-permute-start(f32[10,2,16,128]{3,2,1,0:T(8,128)} %get-tuple-element.37), channel_id=1, source_target_pairs={{0,15},{1,12},{2,13},{3,14},{4,3},{5,0},{6,1},{7,2},{8,7},{9,4},{1... | collective-permute-start | bytes 491528 | tf_op jit(solution)/shard_map/ppermute | solution.py:790
  77.1 31.9 %collective-permute-start.13 = (f32[10,2,16,128]{3,2,1,0:T(8,128)}, f32[10,2,16,128]{3,2,1,0:T(8,128)S(1)}, u32[]{:S(2)}, u32[]{:S(2)}) collective-permute-start(f32[10,2,16,128]{3,2,1,0:T(8,128)} %get-tuple-element.38), channel_id=1, source_target_pairs={{0,9},{1,10},{2,11},{3,8},{4,13},{5,14},{6,15},{7,12},{8,1},{9,2},... | collective-permute-start | bytes 491528 | tf_op jit(solution)/shard_map/ppermute | solution.py:790
  79.5 29.6 %collective-permute-start.14 = (f32[10,2,16,128]{3,2,1,0:T(8,128)}, f32[10,2,16,128]{3,2,1,0:T(8,128)S(1)}, u32[]{:S(2)}, u32[]{:S(2)}) collective-permute-start(f32[10,2,16,128]{3,2,1,0:T(8,128)} %get-tuple-element.39), channel_id=1, source_target_pairs={{0,6},{1,7},{2,4},{3,5},{4,10},{5,11},{6,8},{7,9},{8,14},{9,15},{1... | collective-permute-start | bytes 491528 | tf_op jit(solution)/shard_map/ppermute | solution.py:790
  95.6 36.9 %copy-start.6 = (f32[10,2,16,128]{3,2,1,0:T(8,128)}, f32[10,2,16,128]{3,2,1,0:T(8,128)S(1)}, u32[]{:S(2)}) copy-start(f32[10,2,16,128]{3,2,1,0:T(8,128)S(1)} %collective-permute-done.10.refs_8_) | copy-start | bytes 491524
  95.6 16.1 %collective-permute-start.15 = (f32[10,2,16,128]{3,2,1,0:T(8,128)}, f32[10,2,16,128]{3,2,1,0:T(8,128)S(1)}, u32[]{:S(2)}, u32[]{:S(2)}) collective-permute-start(f32[10,2,16,128]{3,2,1,0:T(8,128)} %get-tuple-element.40), channel_id=1, source_target_pairs={{0,14},{1,15},{2,12},{3,13},{4,2},{5,3},{6,0},{7,1},{8,6},{9,7},{1... | collective-permute-start | bytes 491528 | tf_op jit(solution)/shard_map/ppermute | solution.py:790
  101.1 31.3 %copy-start.7 = (f32[10,2,16,128]{3,2,1,0:T(8,128)}, f32[10,2,16,128]{3,2,1,0:T(8,128)S(1)}, u32[]{:S(2)}) copy-start(f32[10,2,16,128]{3,2,1,0:T(8,128)S(1)} %collective-permute-done.11.refs_9_) | copy-start | bytes 491524
  101.1 16.4 %collective-permute-start.16 = (f32[10,2,16,128]{3,2,1,0:T(8,128)}, f32[10,2,16,128]{3,2,1,0:T(8,128)S(1)}, u32[]{:S(2)}, u32[]{:S(2)}) collective-permute-start(f32[10,2,16,128]{3,2,1,0:T(8,128)} %get-tuple-element.41), channel_id=1, source_target_pairs={{0,11},{1,8},{2,9},{3,10},{4,15},{5,12},{6,13},{7,14},{8,3},{9,0},... | collective-permute-start | bytes 491528 | tf_op jit(solution)/shard_map/ppermute | solution.py:790
  103.3 29.1 %copy-start.8 = (f32[10,2,16,128]{3,2,1,0:T(8,128)}, f32[10,2,16,128]{3,2,1,0:T(8,128)S(1)}, u32[]{:S(2)}) copy-start(f32[10,2,16,128]{3,2,1,0:T(8,128)S(1)} %collective-permute-done.12.refs_10_) | copy-start | bytes 491524
  103.3 15.7 %collective-permute-start.17 = (f32[10,2,16,128]{3,2,1,0:T(8,128)}, f32[10,2,16,128]{3,2,1,0:T(8,128)S(1)}, u32[]{:S(2)}, u32[]{:S(2)}) collective-permute-start(f32[10,2,16,128]{3,2,1,0:T(8,128)} %get-tuple-element.42), channel_id=1, source_target_pairs={{0,10},{1,11},{2,8},{3,9},{4,14},{5,15},{6,12},{7,13},{8,2},{9,3},... | collective-permute-start | bytes 491528 | tf_op jit(solution)/shard_map/ppermute | solution.py:790
  109.0 23.5 %copy-start.9 = (f32[10,2,16,128]{3,2,1,0:T(8,128)}, f32[10,2,16,128]{3,2,1,0:T(8,128)S(1)}, u32[]{:S(2)}) copy-start(f32[10,2,16,128]{3,2,1,0:T(8,128)S(1)} %collective-permute-done.13.refs_11_) | copy-start | bytes 491524
  109.0 12.6 %collective-permute-start.3 = (f32[10,2,16,128]{3,2,1,0:T(8,128)}, f32[10,2,16,128]{3,2,1,0:T(8,128)}, u32[]{:S(2)}, u32[]{:S(2)}) collective-permute-start(f32[10,2,16,128]{3,2,1,0:T(8,128)} %get-tuple-element.28), channel_id=1, source_target_pairs={{0,4},{1,5},{2,6},{3,7},{4,8},{5,9},{6,10},{7,11},{8,12},{9,13},{1... | collective-permute-start | bytes 491528 | tf_op jit(solution)/shard_map/ppermute | solution.py:790
  109.1 23.3 %copy-start.10 = (f32[10,2,16,128]{3,2,1,0:T(8,128)}, f32[10,2,16,128]{3,2,1,0:T(8,128)S(1)}, u32[]{:S(2)}) copy-start(f32[10,2,16,128]{3,2,1,0:T(8,128)S(1)} %collective-permute-done.14.refs_12_) | copy-start | bytes 491524
  109.1 15.2 %collective-permute-start.4 = (f32[10,2,16,128]{3,2,1,0:T(8,128)}, f32[10,2,16,128]{3,2,1,0:T(8,128)}, u32[]{:S(2)}, u32[]{:S(2)}) collective-permute-start(f32[10,2,16,128]{3,2,1,0:T(8,128)} %get-tuple-element.29), channel_id=1, source_target_pairs={{0,12},{1,13},{2,14},{3,15},{4,0},{5,1},{6,2},{7,3},{8,4},{9,5},{1... | collective-permute-start | bytes 491528 | tf_op jit(solution)/shard_map/ppermute | solution.py:790
  111.7 20.8 %copy-start.11 = (f32[10,2,16,128]{3,2,1,0:T(8,128)}, f32[10,2,16,128]{3,2,1,0:T(8,128)S(1)}, u32[]{:S(2)}) copy-start(f32[10,2,16,128]{3,2,1,0:T(8,128)S(1)} %collective-permute-done.15.refs_13_) | copy-start | bytes 491524
  111.7 15.2 %collective-permute-start.5 = (f32[10,2,16,128]{3,2,1,0:T(8,128)}, f32[10,2,16,128]{3,2,1,0:T(8,128)}, u32[]{:S(2)}, u32[]{:S(2)}) collective-permute-start(f32[10,2,16,128]{3,2,1,0:T(8,128)} %get-tuple-element.30), channel_id=1, source_target_pairs={{0,1},{1,2},{2,3},{3,0},{4,5},{5,6},{6,7},{7,4},{8,9},{9,10},{10,1... | collective-permute-start | bytes 491528 | tf_op jit(solution)/shard_map/ppermute | solution.py:790
  117.5 15.0 %copy-start.12 = (f32[10,2,16,128]{3,2,1,0:T(8,128)}, f32[10,2,16,128]{3,2,1,0:T(8,128)S(1)}, u32[]{:S(2)}) copy-start(f32[10,2,16,128]{3,2,1,0:T(8,128)S(1)} %collective-permute-done.16.refs_14_) | copy-start | bytes 491524
  117.5 9.3 %collective-permute-start.6 = (f32[10,2,16,128]{3,2,1,0:T(8,128)}, f32[10,2,16,128]{3,2,1,0:T(8,128)}, u32[]{:S(2)}, u32[]{:S(2)}) collective-permute-start(f32[10,2,16,128]{3,2,1,0:T(8,128)} %get-tuple-element.31), channel_id=1, source_target_pairs={{0,3},{1,0},{2,1},{3,2},{4,7},{5,4},{6,5},{7,6},{8,11},{9,8},{10,9... | collective-permute-start | bytes 491528 | tf_op jit(solution)/shard_map/ppermute | solution.py:790
  119.1 7.8 %collective-permute-start.7 = (f32[10,2,16,128]{3,2,1,0:T(8,128)}, f32[10,2,16,128]{3,2,1,0:T(8,128)}, u32[]{:S(2)}, u32[]{:S(2)}) collective-permute-start(f32[10,2,16,128]{3,2,1,0:T(8,128)} %get-tuple-element.32), channel_id=1, source_target_pairs={{0,8},{1,9},{2,10},{3,11},{4,12},{5,13},{6,14},{7,15},{8,0},{9,1},... | collective-permute-start | bytes 491528 | tf_op jit(solution)/shard_map/ppermute | solution.py:790
  121.6 8.4 %collective-permute-start.8 = (f32[10,2,16,128]{3,2,1,0:T(8,128)}, f32[10,2,16,128]{3,2,1,0:T(8,128)}, u32[]{:S(2)}, u32[]{:S(2)}) collective-permute-start(f32[10,2,16,128]{3,2,1,0:T(8,128)} %get-tuple-element.33), channel_id=1, source_target_pairs={{0,5},{1,6},{2,7},{3,4},{4,9},{5,10},{6,11},{7,8},{8,13},{9,14},{1... | collective-permute-start | bytes 491528 | tf_op jit(solution)/shard_map/ppermute | solution.py:790
  124.4 8.1 %collective-permute-start.9 = (f32[10,2,16,128]{3,2,1,0:T(8,128)}, f32[10,2,16,128]{3,2,1,0:T(8,128)}, u32[]{:S(2)}, u32[]{:S(2)}) collective-permute-start(f32[10,2,16,128]{3,2,1,0:T(8,128)} %get-tuple-element.34), channel_id=1, source_target_pairs={{0,13},{1,14},{2,15},{3,12},{4,1},{5,2},{6,3},{7,0},{8,5},{9,6},{1... | collective-permute-start | bytes 491528 | tf_op jit(solution)/shard_map/ppermute | solution.py:790
  141.8 40.2 %all-to-all-start.2 = ((f32[128,2,16,128]{3,2,1,0:T(8,128)}), f32[128,2,16,128]{3,2,1,0:T(8,128)}, u32[]{:S(2)}, u32[]{:S(2)}) async-start(f32[128,2,16,128]{3,2,1,0:T(8,128)} %shard_map.164), calls=%async_computation.2 | async-start | bytes 4194304 | tf_op jit(solution)/shard_map/all_to_all | solution.py:769
  157.8 20.0 %copy-start.5 = (s32[256]{0:T(256)S(1)}, s32[256]{0:T(256)}, u32[]{:S(2)}) copy-start(s32[256]{0:T(256)} %param.23) | copy-start | bytes 3076
  163.3 24.8 %collective-permute-start.1 = (f32[2112,128]{1,0:T(8,128)}, f32[2112,128]{1,0:T(8,128)S(1)}, u32[]{:S(2)}, u32[]{:S(2)}) collective-permute-start(f32[2112,128]{1,0:T(8,128)} %get-tuple-element.25.refs_2_), channel_id=1, source_target_pairs={{0,16},{16,1},{1,17},{17,5},{5,21},{21,4},{4,20},{20,8},{8,24},{24... | collective-permute-start | bytes 3244040 | tf_op jit(solution)/shard_map/ppermute | solution.py:760
  166.8 21.2 %collective-permute-start.2 = (f32[2112,128]{1,0:T(8,128)S(1)}, f32[2112,128]{1,0:T(8,128)}, u32[]{:S(2)}, u32[]{:S(2)}) collective-permute-start(f32[2112,128]{1,0:T(8,128)S(1)} %get-tuple-element.26.refs_1_), channel_id=1, source_target_pairs={{16,0},{1,16},{17,1},{5,17},{21,5},{4,21},{20,4},{8,20},{24,8},{9,... | collective-permute-start | bytes 3244040 | tf_op jit(solution)/shard_map/ppermute | solution.py:760
  168.8 19.2 %collective-permute-start = (s32[16]{0:T(128)S(1)}, s32[16]{0:T(128)S(1)}, u32[]{:S(2)}, u32[]{:S(2)}) collective-permute-start(s32[16]{0:T(128)S(1)} %pad_add_fusion), channel_id=1, source_target_pairs={{0,0},{1,16},{2,1},{3,17},{4,5},{5,21},{6,4},{7,20},{8,8},{9,24},{... | collective-permute-start | bytes 200 | tf_op jit(solution)/shard_map/ppermute | solution.py:754
  193.5 6.3 %collective-permute-start.18 = (f32[8,512]{1,0:T(8,128)S(1)}, f32[8,512]{1,0:T(8,128)S(1)}, u32[]{:S(2)}, u32[]{:S(2)}) collective-permute-start(f32[8,512]{1,0:T(8,128)S(1)} %get-tuple-element.44), channel_id=1, source_target_pairs={{0,16},{16,0},{1,17},{17,1},{5,21},{21,5},{4,20},{20,4},{8,24},{24... | collective-permute-start | bytes 49160 | tf_op jit(solution)/shard_map/ppermute | solution.py:807
  194.7 7.2 %collective-permute-start.20 = (f32[8,512]{1,0:T(8,128)S(1)}, f32[8,512]{1,0:T(8,128)S(1)}, u32[]{:S(2)}, u32[]{:S(2)}) collective-permute-start(f32[8,512]{1,0:T(8,128)S(1)} %get-tuple-element.44), channel_id=1, source_target_pairs={{16,2},{17,4},{21,6},{20,8},{24,10},{25,12},{29,14},{28,16},{31,18... | collective-permute-start | bytes 49160 | tf_op jit(solution)/shard_map/ppermute | solution.py:808
  199.8 8.6 %collective-permute-start.19 = (f32[16,512]{1,0:T(8,128)S(1)}, f32[16,512]{1,0:T(8,128)S(1)}, u32[]{:S(2)}, u32[]{:S(2)}) collective-permute-start(f32[16,512]{1,0:T(8,128)S(1)} %merge.1), channel_id=1, source_target_pairs={{0,0},{16,1},{1,2},{17,3},{5,4},{21,5},{4,6},{20,7},{8,8},{24,9},{... | collective-permute-start | bytes 98312 | tf_op jit(solution)/shard_map/ppermute | solution.py:815
  (6 other events, 62.8 us)

commit v3 on v2

--- a/solution.py
+++ b/solution.py
@@ -25,10 +25,10 @@
 BF16 = jnp.bfloat16
 
 
-SHIFTS = sorted(
-    ((dx, dz) for dx in range(4) for dz in range(4)),
-    key=lambda s: min(s[0], 4 - s[0]) + min(s[1], 4 - s[1]),
-)
+SHIFTS = [
+    (0, 0), (1, 0), (0, 1), (3, 0), (0, 3), (2, 0), (0, 2), (1, 1), (3, 3),
+    (1, 3), (3, 1), (2, 1), (1, 2), (2, 3), (3, 2), (2, 2),
+]
 
 
 def shifted(r, shift):
@@ -258,7 +258,7 @@
 
 
 PRE_SCRATCH = [
-    pltpu.VMEM((5000, 128), F32),
+    pltpu.VMEM((5016, 128), F32),
     pltpu.VMEM((NP, NQ, 2, 16, 128), F32),
     pltpu.SemaphoreType.DMA((5 + NP,)),
 ]
@@ -336,7 +336,7 @@
             d_ref[at, 1] = i
         return carry
 
-    lax.fori_loop(0, NP, middle, 0, unroll=8)
+    lax.fori_loop(0, NP, middle, 0, unroll=16)
 
     def inner(q, carry):
         for g in range(2):
@@ -351,7 +351,7 @@
     lax.fori_loop(0, NQ, inner, 0, unroll=2)
 
     def store(part):
-        at = pl.ds(32 * part, 32)
+        at = (pl.ds(2 * (part // 2), 2), slice(None), part % 2)
         return pltpu.make_async_copy(o_ref.at[at], o_hbm.at[at], out_sem.at[part])
 
     for d in range(128):
@@ -367,10 +367,11 @@
                 nxt = pltpu.roll(nxt, start % 128, 1)
                 val = jnp.where(lane < start, val, nxt)
                 start += NS
-            o_ref[worker(d), c] = val
-        if d % 32 == 31:
-            store(d // 32).start()
-    for part in range(4):
+            az, rg = divmod(worker(d), 16)
+            o_ref[az, rg // 4, rg % 4 // 2, rg % 2, c] = val
+        if d % 16 == 15:
+            store(d // 16).start()
+    for part in range(8):
         store(part).wait()
 
 
@@ -435,18 +436,18 @@
         kernel,
         in_specs=specs + [HBM] * 7,
         out_specs=HBM,
-        out_shape=jax.ShapeDtypeStruct((128, 2, 16, 128), F32),
+        out_shape=jax.ShapeDtypeStruct((8, 4, 2, 2, 2, 16, 128), F32),
         scratch_shapes=[pltpu.VMEM(x.shape, x.dtype) for x in tables]
         + [
             pltpu.VMEM((NP * NQ, 2, 16, 128), F32),
             pltpu.VMEM((NP, NQ, 2, 16, 128), F32),
-            pltpu.VMEM((128, 2, 16, 128), F32),
-            pltpu.SemaphoreType.DMA((4,)),
+            pltpu.VMEM((8, 4, 2, 2, 2, 16, 128), F32),
+            pltpu.SemaphoreType.DMA((8,)),
             pltpu.SemaphoreType.DMA((NP,)),
             pltpu.SemaphoreType.DMA((7,)),
         ],
         cost_estimate=pl.CostEstimate(flops=10**10, bytes_accessed=6 * 10**6, transcendentals=0),
-    )(*operands, *tables)
+    )(*operands, *tables).reshape(128, 2, 16, 128)
 
 
 def _dot_t(a, b):
@@ -702,7 +703,7 @@
             jax.ShapeDtypeStruct((8, 512), F32),
         ),
         scratch_shapes=[
-            pltpu.VMEM((4, LINES + 2 * ASH, 128), F32),
+            pltpu.VMEM((4, LINES + 2 * ASH + 16, 128), F32),
             pltpu.VMEM((2, LINES, 128), F32),
             pltpu.VMEM((512, 128), F32),
             pltpu.SemaphoreType.DMA((20,)),

time: 210 us -> 211 us (level)
  starting transfers between devices: 81 us -> 83.2 us
where the time goes in v3:
time: 211 us
  starting transfers between devices  83.2 us (39%)
  waiting for transfers between devices  75.6 us (36%)
  Pallas kernels  45 us (21%)
  local copies, waits for them, and re-layouts  4.6 us (2%)
    all_to_all x1, waiting for transfers between devices, local(): slave = lax.all_to_all(slave, 'rg', 0, 0, tiled=True)  36.8 us
    ppermute x15, starting transfers between devices, local(): lax.ppermute(piece, 'rg', [(r, shifted(r, shift)) for r in range(NP)])  33 us
    ppermute x15, waiting for transfers between devices, local(): lax.ppermute(piece, 'rg', [(r, shifted(r, shift)) for r in range(NP)])  30.4 us
    all_to_all x2, starting transfers between devices, columns_of(): return lax.all_to_all(ranged, ALL, 0, 0, tiled=True)  19.1 us
    pallas_call x2, Pallas kernels, range_compress(): pl.pallas_call(kernel, in_specs=specs + [HBM] * 7, out_specs=HBM, out_sha...  16.8 us
    ppermute x1, starting transfers between devices, to_worker(): return lax.ppermute(x, ALL, [(b, worker(b)) for b in range(128)])  8.87 us
    all_to_all x1, starting transfers between devices, local(): slave = lax.all_to_all(slave, 'rg', 0, 0, tiled=True)  8.6 us
    ppermute x1, waiting for transfers between devices, local(): box = lax.ppermute(box, ALL, [(worker(b), b) for b in range(128)])  6.5 us
  transfers between devices with their start and end apart: 24, of which 11 were waited for; matrix products, arithmetic and copies ran while one was open for 3% of the time, Pallas kernels for 13%

profile of v3, /device:TPU:1, one launch (start us, length us, event | category | flops | bytes accessed | tf_op | source)
XLA Modules:
  0.0 210.6 jit_solution(16288154436419071566)
XLA Ops:
  0.0 3.1 %pre.1 = f32[16,10,2,16,128]{4,3,2,1,0:T(8,128)} custom-call(f32[5000,128]{1,0:T(8,128)} %bitcast.27), custom_call_target="tpu_custom_call" | custom-call | flops 100000000 | bytes 10000000 | tf_op jit(solution)/shard_map/pre/pallas_call | solution.py:268
  3.2 8.6 %all-to-all-start = ((f32[16,10,2,16,128]{4,3,2,1,0:T(8,128)}), f32[16,10,2,16,128]{4,3,2,1,0:T(8,128)}, u32[]{:S(2)}, u32[]{:S(2)}) async-start(f32[16,10,2,16,128]{4,3,2,1,0:T(8,128)} %pre.1), calls=%async_computation | async-start | bytes 5242880 | tf_op jit(solution)/shard_map/all_to_all | solution.py:787
  14.1 36.8 %all-to-all-done.x_hbm = f32[16,10,2,16,128]{4,3,2,1,0:T(8,128)} async-done(((f32[16,10,2,16,128]{4,3,2,1,0:T(8,128)}), f32[16,10,2,16,128]{4,3,2,1,0:T(8,128)}, u32[]{:S(2)}, u32[]{:S(2)}) %all-to-all-start) | async-done | bytes 2621472 | tf_op jit(solution)/shard_map/all_to_all | solution.py:787
  50.9 8.0 %shard_map.163 = f32[8,4,2,2,2,16,128]{6,5,4,3,2,1,0:T(8,128)} custom-call(f32[16,10,2,16,128]{4,3,2,1,0:T(8,128)} %all-to-all-done.x_hbm, f32[10,2,128]{2,1,0:T(2,128)} %constant.113.clone.refs_0_.refs_16_, f32[160,2,128]{2,1,0:T(2,128)} %pad.8.refs_1_.refs_17_, bf16[256,256]{1,0:T(8,128)(2,1)} %constant.114.clone.refs_2_.refs_18_, ...), custom_call_target="tpu_custom_call" | custom-call | flops 10000000000 | bytes 6000000 | tf_op jit(solution)/shard_map/pallas_call | solution.py:435
  58.9 7.5 %all-to-all-start.1 = ((f32[128,2,16,128]{3,2,1,0:T(8,128)}), f32[128,2,16,128]{3,2,1,0:T(8,128)S(1)}, u32[]{:S(2)}, u32[]{:S(2)}) async-start(f32[128,2,16,128]{3,2,1,0:T(8,128)} %bitcast.30), calls=%async_computation.1 | async-start | bytes 4194304 | tf_op jit(solution)/shard_map/all_to_all | solution.py:770
  66.4 3.8 %pre_shifts.1 = (f32[10,2,16,128]{3,2,1,0:T(8,128)}, f32[10,2,16,128]{3,2,1,0:T(8,128)}, f32[10,2,16,128]{3,2,1,0:T(8,128)}, f32[10,2,16,128]{3,2,1,0:T(8,128)},...) custom-call(s32[1]{0:T(128)} %bitcast.11.me_ref, ...), custom_call_target="tpu_custom_call" | custom-call | flops 100000000 | bytes 10000000 | tf_op jit(solution)/shard_map/pre_shifts/pallas_call | solution.py:280
  70.2 5.5 %collective-permute-start.10 = (f32[10,2,16,128]{3,2,1,0:T(8,128)}, f32[10,2,16,128]{3,2,1,0:T(8,128)S(1)}, u32[]{:S(2)}, u32[]{:S(2)}) collective-permute-start(f32[10,2,16,128]{3,2,1,0:T(8,128)} %get-tuple-element.35), channel_id=1, source_target_pairs={{0,15},{1,12},{2,13},{3,14},{4,3},{5,0},{6,1},{7,2},{8,7},{9,4},{1... | collective-permute-start | bytes 491528 | tf_op jit(solution)/shard_map/ppermute | solution.py:791
  75.6 3.6 %collective-permute-start.12 = (f32[10,2,16,128]{3,2,1,0:T(8,128)}, f32[10,2,16,128]{3,2,1,0:T(8,128)S(1)}, u32[]{:S(2)}, u32[]{:S(2)}) collective-permute-start(f32[10,2,16,128]{3,2,1,0:T(8,128)} %get-tuple-element.37), channel_id=1, source_target_pairs={{0,7},{1,4},{2,5},{3,6},{4,11},{5,8},{6,9},{7,10},{8,15},{9,12},{1... | collective-permute-start | bytes 491528 | tf_op jit(solution)/shard_map/ppermute | solution.py:791
  79.2 2.1 collective-permute-start.14
  81.2 17.6 %collective-permute-done.10.refs_8_ = f32[10,2,16,128]{3,2,1,0:T(8,128)S(1)} collective-permute-done((f32[10,2,16,128]{3,2,1,0:T(8,128)}, f32[10,2,16,128]{3,2,1,0:T(8,128)S(1)}, u32[]{:S(2)}, u32[]{:S(2)}) %collective-permute-start.10) | collective-permute-done | bytes 163872 | tf_op jit(solution)/shard_map/ppermute | solution.py:791
  98.9 3.4 %collective-permute-start.15 = (f32[10,2,16,128]{3,2,1,0:T(8,128)}, f32[10,2,16,128]{3,2,1,0:T(8,128)S(1)}, u32[]{:S(2)}, u32[]{:S(2)}) collective-permute-start(f32[10,2,16,128]{3,2,1,0:T(8,128)} %get-tuple-element.40), channel_id=1, source_target_pairs={{0,14},{1,15},{2,12},{3,13},{4,2},{5,3},{6,0},{7,1},{8,6},{9,7},{1... | collective-permute-start | bytes 491528 | tf_op jit(solution)/shard_map/ppermute | solution.py:791
  102.3 3.0 %collective-permute-start.16 = (f32[10,2,16,128]{3,2,1,0:T(8,128)}, f32[10,2,16,128]{3,2,1,0:T(8,128)S(1)}, u32[]{:S(2)}, u32[]{:S(2)}) collective-permute-start(f32[10,2,16,128]{3,2,1,0:T(8,128)} %get-tuple-element.41), channel_id=1, source_target_pairs={{0,11},{1,8},{2,9},{3,10},{4,15},{5,12},{6,13},{7,14},{8,3},{9,0},... | collective-permute-start | bytes 491528 | tf_op jit(solution)/shard_map/ppermute | solution.py:791
  106.3 3.0 %collective-permute-start.17 = (f32[10,2,16,128]{3,2,1,0:T(8,128)}, f32[10,2,16,128]{3,2,1,0:T(8,128)S(1)}, u32[]{:S(2)}, u32[]{:S(2)}) collective-permute-start(f32[10,2,16,128]{3,2,1,0:T(8,128)} %get-tuple-element.42), channel_id=1, source_target_pairs={{0,10},{1,11},{2,8},{3,9},{4,14},{5,15},{6,12},{7,13},{8,2},{9,3},... | collective-permute-start | bytes 491528 | tf_op jit(solution)/shard_map/ppermute | solution.py:791
  109.3 5.4 %collective-permute-start.3 = (f32[10,2,16,128]{3,2,1,0:T(8,128)}, f32[10,2,16,128]{3,2,1,0:T(8,128)}, u32[]{:S(2)}, u32[]{:S(2)}) collective-permute-start(f32[10,2,16,128]{3,2,1,0:T(8,128)} %get-tuple-element.28), channel_id=1, source_target_pairs={{0,1},{1,2},{2,3},{3,0},{4,5},{5,6},{6,7},{7,4},{8,9},{9,10},{10,1... | collective-permute-start | bytes 491528 | tf_op jit(solution)/shard_map/ppermute | solution.py:791
  114.8 3.9 %collective-permute-done.16.refs_14_ = f32[10,2,16,128]{3,2,1,0:T(8,128)S(1)} collective-permute-done((f32[10,2,16,128]{3,2,1,0:T(8,128)}, f32[10,2,16,128]{3,2,1,0:T(8,128)S(1)}, u32[]{:S(2)}, u32[]{:S(2)}) %collective-permute-start.16) | collective-permute-done | bytes 163872 | tf_op jit(solution)/shard_map/ppermute | solution.py:791
  118.7 1.8 collective-permute-start.6
  120.5 2.9 %collective-permute-start.7 = (f32[10,2,16,128]{3,2,1,0:T(8,128)}, f32[10,2,16,128]{3,2,1,0:T(8,128)}, u32[]{:S(2)}, u32[]{:S(2)}) collective-permute-start(f32[10,2,16,128]{3,2,1,0:T(8,128)} %get-tuple-element.32), channel_id=1, source_target_pairs={{0,2},{1,3},{2,0},{3,1},{4,6},{5,7},{6,4},{7,5},{8,10},{9,11},{10,... | collective-permute-start | bytes 491528 | tf_op jit(solution)/shard_map/ppermute | solution.py:791
  124.8 1.6 collective-permute-start.9
  126.5 3.0 %collective-permute-done.8.refs_6_ = f32[10,2,16,128]{3,2,1,0:T(8,128)} collective-permute-done((f32[10,2,16,128]{3,2,1,0:T(8,128)}, f32[10,2,16,128]{3,2,1,0:T(8,128)}, u32[]{:S(2)}, u32[]{:S(2)}) %collective-permute-start.8) | collective-permute-done | bytes 163872 | tf_op jit(solution)/shard_map/ppermute | solution.py:791
  129.5 4.2 %collective-permute-done.9.refs_7_ = f32[10,2,16,128]{3,2,1,0:T(8,128)} collective-permute-done((f32[10,2,16,128]{3,2,1,0:T(8,128)}, f32[10,2,16,128]{3,2,1,0:T(8,128)}, u32[]{:S(2)}, u32[]{:S(2)}) %collective-permute-start.9) | collective-permute-done | bytes 163872 | tf_op jit(solution)/shard_map/ppermute | solution.py:791
  133.7 8.9 %shard_map.164 = f32[8,4,2,2,2,16,128]{6,5,4,3,2,1,0:T(8,128)} custom-call(s32[1]{0:T(128)} %bitcast.11.me_ref, f32[10,2,16,128]{3,2,1,0:T(8,128)} %get-tuple-element.27.refs_0_, f32[10,2,16,128]{3,2,1,0:T(8,128)} %collective-permute-done.3.refs_1_, f32[10,2,16,128]{3,2,1,0:T(8,128)} %collective-permute-done.4.refs_2_, ...), custom_call_target="tpu_custom_call" | custom-call | flops 10000000000 | bytes 6000000 | tf_op jit(solution)/shard_map/pallas_call | solution.py:435
  142.6 11.6 %all-to-all-start.2 = ((f32[128,2,16,128]{3,2,1,0:T(8,128)}), f32[128,2,16,128]{3,2,1,0:T(8,128)}, u32[]{:S(2)}, u32[]{:S(2)}) async-start(f32[128,2,16,128]{3,2,1,0:T(8,128)} %bitcast.29), calls=%async_computation.2 | async-start | bytes 4194304 | tf_op jit(solution)/shard_map/all_to_all | solution.py:770
  155.4 3.9 %prep.1.a_hbm = bf16[16,256,256]{2,1,0:T(8,128)(2,1)} custom-call(f32[2,16,128]{2,1,0:T(8,128)} %bitcast.32, f32[2,128,128]{2,1,0:T(8,128)} %constant.119.clone.dft_ref, f32[2,16,128]{2,1,0:T(8,128)} %constant.120.clone.turn_ref, f32[16,2,128]{2,1,0:T(2,128)} %constant.121.clone.wrap_ref), custom_call_target="tpu_custom_call" | custom-call | flops 2000000000 | bytes 5000000 | tf_op jit(solution)/shard_map/prep/pallas_call | solution.py:493
  159.4 5.4 %slave_azimuth.1 = (f32[2112,128]{1,0:T(8,128)S(1)}, f32[2112,128]{1,0:T(8,128)}) custom-call(f32[16,8,2,16,128]{4,3,2,1,0:T(8,128)S(1)} %bitcast.25, bf16[16,256,256]{2,1,0:T(8,128)(2,1)} %prep.1.a_hbm), custom_call_target="tpu_custom_call" | custom-call | flops 5000000000 | bytes 10000000 | tf_op jit(solution)/shard_map/slave_azimuth/pallas_call | solution.py:593
  164.8 3.5 %collective-permute-start.1 = (f32[2112,128]{1,0:T(8,128)}, f32[2112,128]{1,0:T(8,128)S(1)}, u32[]{:S(2)}, u32[]{:S(2)}) collective-permute-start(f32[2112,128]{1,0:T(8,128)} %get-tuple-element.25.refs_2_), channel_id=1, source_target_pairs={{0,16},{16,1},{1,17},{17,5},{5,21},{21,4},{4,20},{20,8},{8,24},{24... | collective-permute-start | bytes 3244040 | tf_op jit(solution)/shard_map/ppermute | solution.py:761
  168.4 1.9 collective-permute-start.2
  170.4 8.9 %collective-permute-start = (s32[16]{0:T(128)S(1)}, s32[16]{0:T(128)S(1)}, u32[]{:S(2)}, u32[]{:S(2)}) collective-permute-start(s32[16]{0:T(128)S(1)} %pad_add_fusion), channel_id=1, source_target_pairs={{0,0},{1,16},{2,1},{3,17},{4,5},{5,21},{6,4},{7,20},{8,8},{9,24},{... | collective-permute-start | bytes 200 | tf_op jit(solution)/shard_map/ppermute | solution.py:755
  183.5 5.8 %master_azimuth.1.refs_4_ = f32[2,2048,128]{2,1,0:T(8,128)} custom-call(f32[16,8,2,16,128]{4,3,2,1,0:T(8,128)} %bitcast.17.x_hbm, bf16[16,256,256]{2,1,0:T(8,128)(2,1)} %prep.1.a_hbm), custom_call_target="tpu_custom_call" | custom-call | flops 5000000000 | bytes 10000000 | tf_op jit(solution)/shard_map/master_azimuth/pallas_call | solution.py:624
  189.6 5.5 %looks.1 = (f32[16,512]{1,0:T(8,128)S(1)}, f32[8,512]{1,0:T(8,128)S(1)}) custom-call(s32[16]{0:T(128)S(1)} %collective-permute-done.shift_ref, f32[2112,128]{1,0:T(8,128)S(1)} %collective-permute-done.1.refs_0_, f32[2112,128]{1,0:T(8,128)S(1)} %get-tuple-element.26.refs_1_, f32[2112,128]{1,0:T(8,128)} %get-tuple-element.25.refs_2_, ...), custom_call_target="tpu_custom_call" | custom-call | flops 5000000000 | bytes 10000000 | tf_op jit(solution)/shard_map/looks/pallas_call | solution.py:698
  196.2 5.2 %collective-permute-start.20 = (f32[8,512]{1,0:T(8,128)S(1)}, f32[8,512]{1,0:T(8,128)S(1)}, u32[]{:S(2)}, u32[]{:S(2)}) collective-permute-start(f32[8,512]{1,0:T(8,128)S(1)} %get-tuple-element.44), channel_id=1, source_target_pairs={{16,2},{17,4},{21,6},{20,8},{24,10},{25,12},{29,14},{28,16},{31,18... | collective-permute-start | bytes 49160 | tf_op jit(solution)/shard_map/ppermute | solution.py:809
  201.4 1.9 collective-permute-start.19
  203.5 6.5 %collective-permute-done.19.box_ref = f32[16,512]{1,0:T(8,128)S(1)} collective-permute-done((f32[16,512]{1,0:T(8,128)S(1)}, f32[16,512]{1,0:T(8,128)S(1)}, u32[]{:S(2)}, u32[]{:S(2)}) %collective-permute-start.19) | collective-permute-done | bytes 32800 | tf_op jit(solution)/shard_map/ppermute | solution.py:816
  (79 shorter events, 12.5 us)
Async XLA Ops:
  3.2 47.7 %all-to-all-start = ((f32[16,10,2,16,128]{4,3,2,1,0:T(8,128)}), f32[16,10,2,16,128]{4,3,2,1,0:T(8,128)}, u32[]{:S(2)}, u32[]{:S(2)}) async-start(f32[16,10,2,16,128]{4,3,2,1,0:T(8,128)} %pre.1), calls=%async_computation | async-start | bytes 5242880 | tf_op jit(solution)/shard_map/all_to_all | solution.py:787
  58.9 83.7 %all-to-all-start.1 = ((f32[128,2,16,128]{3,2,1,0:T(8,128)}), f32[128,2,16,128]{3,2,1,0:T(8,128)S(1)}, u32[]{:S(2)}, u32[]{:S(2)}) async-start(f32[128,2,16,128]{3,2,1,0:T(8,128)} %bitcast.30), calls=%async_computation.1 | async-start | bytes 4194304 | tf_op jit(solution)/shard_map/all_to_all | solution.py:770
  70.2 28.7 %collective-permute-start.10 = (f32[10,2,16,128]{3,2,1,0:T(8,128)}, f32[10,2,16,128]{3,2,1,0:T(8,128)S(1)}, u32[]{:S(2)}, u32[]{:S(2)}) collective-permute-start(f32[10,2,16,128]{3,2,1,0:T(8,128)} %get-tuple-element.35), channel_id=1, source_target_pairs={{0,15},{1,12},{2,13},{3,14},{4,3},{5,0},{6,1},{7,2},{8,7},{9,4},{1... | collective-permute-start | bytes 491528 | tf_op jit(solution)/shard_map/ppermute | solution.py:791
  75.6 26.7 %collective-permute-start.11 = (f32[10,2,16,128]{3,2,1,0:T(8,128)}, f32[10,2,16,128]{3,2,1,0:T(8,128)S(1)}, u32[]{:S(2)}, u32[]{:S(2)}) collective-permute-start(f32[10,2,16,128]{3,2,1,0:T(8,128)} %get-tuple-element.36), channel_id=1, source_target_pairs={{0,13},{1,14},{2,15},{3,12},{4,1},{5,2},{6,3},{7,0},{8,5},{9,6},{1... | collective-permute-start | bytes 491528 | tf_op jit(solution)/shard_map/ppermute | solution.py:791
  75.6 30.7 %collective-permute-start.12 = (f32[10,2,16,128]{3,2,1,0:T(8,128)}, f32[10,2,16,128]{3,2,1,0:T(8,128)S(1)}, u32[]{:S(2)}, u32[]{:S(2)}) collective-permute-start(f32[10,2,16,128]{3,2,1,0:T(8,128)} %get-tuple-element.37), channel_id=1, source_target_pairs={{0,7},{1,4},{2,5},{3,6},{4,11},{5,8},{6,9},{7,10},{8,15},{9,12},{1... | collective-permute-start | bytes 491528 | tf_op jit(solution)/shard_map/ppermute | solution.py:791
  79.2 30.1 %collective-permute-start.13 = (f32[10,2,16,128]{3,2,1,0:T(8,128)}, f32[10,2,16,128]{3,2,1,0:T(8,128)S(1)}, u32[]{:S(2)}, u32[]{:S(2)}) collective-permute-start(f32[10,2,16,128]{3,2,1,0:T(8,128)} %get-tuple-element.38), channel_id=1, source_target_pairs={{0,6},{1,7},{2,4},{3,5},{4,10},{5,11},{6,8},{7,9},{8,14},{9,15},{1... | collective-permute-start | bytes 491528 | tf_op jit(solution)/shard_map/ppermute | solution.py:791
  79.2 35.5 %collective-permute-start.14 = (f32[10,2,16,128]{3,2,1,0:T(8,128)}, f32[10,2,16,128]{3,2,1,0:T(8,128)S(1)}, u32[]{:S(2)}, u32[]{:S(2)}) collective-permute-start(f32[10,2,16,128]{3,2,1,0:T(8,128)} %get-tuple-element.39), channel_id=1, source_target_pairs={{0,9},{1,10},{2,11},{3,8},{4,13},{5,14},{6,15},{7,12},{8,1},{9,2},... | collective-permute-start | bytes 491528 | tf_op jit(solution)/shard_map/ppermute | solution.py:791
  98.9 34.8 %copy-start.6 = (f32[10,2,16,128]{3,2,1,0:T(8,128)}, f32[10,2,16,128]{3,2,1,0:T(8,128)S(1)}, u32[]{:S(2)}) copy-start(f32[10,2,16,128]{3,2,1,0:T(8,128)S(1)} %collective-permute-done.10.refs_8_) | copy-start | bytes 491524
  98.9 15.8 %collective-permute-start.15 = (f32[10,2,16,128]{3,2,1,0:T(8,128)}, f32[10,2,16,128]{3,2,1,0:T(8,128)S(1)}, u32[]{:S(2)}, u32[]{:S(2)}) collective-permute-start(f32[10,2,16,128]{3,2,1,0:T(8,128)} %get-tuple-element.40), channel_id=1, source_target_pairs={{0,14},{1,15},{2,12},{3,13},{4,2},{5,3},{6,0},{7,1},{8,6},{9,7},{1... | collective-permute-start | bytes 491528 | tf_op jit(solution)/shard_map/ppermute | solution.py:791
  102.3 31.3 %copy-start.7 = (f32[10,2,16,128]{3,2,1,0:T(8,128)}, f32[10,2,16,128]{3,2,1,0:T(8,128)S(1)}, u32[]{:S(2)}) copy-start(f32[10,2,16,128]{3,2,1,0:T(8,128)S(1)} %collective-permute-done.11.refs_9_) | copy-start | bytes 491524
  102.3 16.3 %collective-permute-start.16 = (f32[10,2,16,128]{3,2,1,0:T(8,128)}, f32[10,2,16,128]{3,2,1,0:T(8,128)S(1)}, u32[]{:S(2)}, u32[]{:S(2)}) collective-permute-start(f32[10,2,16,128]{3,2,1,0:T(8,128)} %get-tuple-element.41), channel_id=1, source_target_pairs={{0,11},{1,8},{2,9},{3,10},{4,15},{5,12},{6,13},{7,14},{8,3},{9,0},... | collective-permute-start | bytes 491528 | tf_op jit(solution)/shard_map/ppermute | solution.py:791
  106.3 27.3 %copy-start.8 = (f32[10,2,16,128]{3,2,1,0:T(8,128)}, f32[10,2,16,128]{3,2,1,0:T(8,128)S(1)}, u32[]{:S(2)}) copy-start(f32[10,2,16,128]{3,2,1,0:T(8,128)S(1)} %collective-permute-done.12.refs_10_) | copy-start | bytes 491524
  106.3 14.2 %collective-permute-start.17 = (f32[10,2,16,128]{3,2,1,0:T(8,128)}, f32[10,2,16,128]{3,2,1,0:T(8,128)S(1)}, u32[]{:S(2)}, u32[]{:S(2)}) collective-permute-start(f32[10,2,16,128]{3,2,1,0:T(8,128)} %get-tuple-element.42), channel_id=1, source_target_pairs={{0,10},{1,11},{2,8},{3,9},{4,14},{5,15},{6,12},{7,13},{8,2},{9,3},... | collective-permute-start | bytes 491528 | tf_op jit(solution)/shard_map/ppermute | solution.py:791
  109.3 24.3 %copy-start.9 = (f32[10,2,16,128]{3,2,1,0:T(8,128)}, f32[10,2,16,128]{3,2,1,0:T(8,128)S(1)}, u32[]{:S(2)}) copy-start(f32[10,2,16,128]{3,2,1,0:T(8,128)S(1)} %collective-permute-done.13.refs_11_) | copy-start | bytes 491524
  109.3 14.1 %collective-permute-start.3 = (f32[10,2,16,128]{3,2,1,0:T(8,128)}, f32[10,2,16,128]{3,2,1,0:T(8,128)}, u32[]{:S(2)}, u32[]{:S(2)}) collective-permute-start(f32[10,2,16,128]{3,2,1,0:T(8,128)} %get-tuple-element.28), channel_id=1, source_target_pairs={{0,1},{1,2},{2,3},{3,0},{4,5},{5,6},{6,7},{7,4},{8,9},{9,10},{10,1... | collective-permute-start | bytes 491528 | tf_op jit(solution)/shard_map/ppermute | solution.py:791
  114.7 19.0 %copy-start.10 = (f32[10,2,16,128]{3,2,1,0:T(8,128)}, f32[10,2,16,128]{3,2,1,0:T(8,128)S(1)}, u32[]{:S(2)}) copy-start(f32[10,2,16,128]{3,2,1,0:T(8,128)S(1)} %collective-permute-done.14.refs_12_) | copy-start | bytes 491524
  114.7 10.1 %collective-permute-start.4 = (f32[10,2,16,128]{3,2,1,0:T(8,128)}, f32[10,2,16,128]{3,2,1,0:T(8,128)}, u32[]{:S(2)}, u32[]{:S(2)}) collective-permute-start(f32[10,2,16,128]{3,2,1,0:T(8,128)} %get-tuple-element.29), channel_id=1, source_target_pairs={{0,4},{1,5},{2,6},{3,7},{4,8},{5,9},{6,10},{7,11},{8,12},{9,13},{1... | collective-permute-start | bytes 491528 | tf_op jit(solution)/shard_map/ppermute | solution.py:791
  114.7 19.0 %copy-start.11 = (f32[10,2,16,128]{3,2,1,0:T(8,128)}, f32[10,2,16,128]{3,2,1,0:T(8,128)S(1)}, u32[]{:S(2)}) copy-start(f32[10,2,16,128]{3,2,1,0:T(8,128)S(1)} %collective-permute-done.15.refs_13_) | copy-start | bytes 491524
  114.7 11.7 %collective-permute-start.5 = (f32[10,2,16,128]{3,2,1,0:T(8,128)}, f32[10,2,16,128]{3,2,1,0:T(8,128)}, u32[]{:S(2)}, u32[]{:S(2)}) collective-permute-start(f32[10,2,16,128]{3,2,1,0:T(8,128)} %get-tuple-element.30), channel_id=1, source_target_pairs={{0,3},{1,0},{2,1},{3,2},{4,7},{5,4},{6,5},{7,6},{8,11},{9,8},{10,9... | collective-permute-start | bytes 491528 | tf_op jit(solution)/shard_map/ppermute | solution.py:791
  118.7 15.0 %copy-start.12 = (f32[10,2,16,128]{3,2,1,0:T(8,128)}, f32[10,2,16,128]{3,2,1,0:T(8,128)S(1)}, u32[]{:S(2)}) copy-start(f32[10,2,16,128]{3,2,1,0:T(8,128)S(1)} %collective-permute-done.16.refs_14_) | copy-start | bytes 491524
  118.7 7.8 %collective-permute-start.6 = (f32[10,2,16,128]{3,2,1,0:T(8,128)}, f32[10,2,16,128]{3,2,1,0:T(8,128)}, u32[]{:S(2)}, u32[]{:S(2)}) collective-permute-start(f32[10,2,16,128]{3,2,1,0:T(8,128)} %get-tuple-element.31), channel_id=1, source_target_pairs={{0,12},{1,13},{2,14},{3,15},{4,0},{5,1},{6,2},{7,3},{8,4},{9,5},{1... | collective-permute-start | bytes 491528 | tf_op jit(solution)/shard_map/ppermute | solution.py:791
  120.5 6.0 %collective-permute-start.7 = (f32[10,2,16,128]{3,2,1,0:T(8,128)}, f32[10,2,16,128]{3,2,1,0:T(8,128)}, u32[]{:S(2)}, u32[]{:S(2)}) collective-permute-start(f32[10,2,16,128]{3,2,1,0:T(8,128)} %get-tuple-element.32), channel_id=1, source_target_pairs={{0,2},{1,3},{2,0},{3,1},{4,6},{5,7},{6,4},{7,5},{8,10},{9,11},{10,... | collective-permute-start | bytes 491528 | tf_op jit(solution)/shard_map/ppermute | solution.py:791
  123.4 6.1 %collective-permute-start.8 = (f32[10,2,16,128]{3,2,1,0:T(8,128)}, f32[10,2,16,128]{3,2,1,0:T(8,128)}, u32[]{:S(2)}, u32[]{:S(2)}) collective-permute-start(f32[10,2,16,128]{3,2,1,0:T(8,128)} %get-tuple-element.33), channel_id=1, source_target_pairs={{0,8},{1,9},{2,10},{3,11},{4,12},{5,13},{6,14},{7,15},{8,0},{9,1},... | collective-permute-start | bytes 491528 | tf_op jit(solution)/shard_map/ppermute | solution.py:791
  124.8 8.8 %collective-permute-start.9 = (f32[10,2,16,128]{3,2,1,0:T(8,128)}, f32[10,2,16,128]{3,2,1,0:T(8,128)}, u32[]{:S(2)}, u32[]{:S(2)}) collective-permute-start(f32[10,2,16,128]{3,2,1,0:T(8,128)} %get-tuple-element.34), channel_id=1, source_target_pairs={{0,5},{1,6},{2,7},{3,4},{4,9},{5,10},{6,11},{7,8},{8,13},{9,14},{1... | collective-permute-start | bytes 491528 | tf_op jit(solution)/shard_map/ppermute | solution.py:791
  142.6 40.9 %all-to-all-start.2 = ((f32[128,2,16,128]{3,2,1,0:T(8,128)}), f32[128,2,16,128]{3,2,1,0:T(8,128)}, u32[]{:S(2)}, u32[]{:S(2)}) async-start(f32[128,2,16,128]{3,2,1,0:T(8,128)} %bitcast.29), calls=%async_computation.2 | async-start | bytes 4194304 | tf_op jit(solution)/shard_map/all_to_all | solution.py:770
  159.4 20.0 %copy-start.5 = (s32[256]{0:T(256)S(1)}, s32[256]{0:T(256)}, u32[]{:S(2)}) copy-start(s32[256]{0:T(256)} %param.23) | copy-start | bytes 3076
  164.8 24.8 %collective-permute-start.1 = (f32[2112,128]{1,0:T(8,128)}, f32[2112,128]{1,0:T(8,128)S(1)}, u32[]{:S(2)}, u32[]{:S(2)}) collective-permute-start(f32[2112,128]{1,0:T(8,128)} %get-tuple-element.25.refs_2_), channel_id=1, source_target_pairs={{0,16},{16,1},{1,17},{17,5},{5,21},{21,4},{4,20},{20,8},{8,24},{24... | collective-permute-start | bytes 3244040 | tf_op jit(solution)/shard_map/ppermute | solution.py:761
  168.4 21.2 %collective-permute-start.2 = (f32[2112,128]{1,0:T(8,128)S(1)}, f32[2112,128]{1,0:T(8,128)}, u32[]{:S(2)}, u32[]{:S(2)}) collective-permute-start(f32[2112,128]{1,0:T(8,128)S(1)} %get-tuple-element.26.refs_1_), channel_id=1, source_target_pairs={{16,0},{1,16},{17,1},{5,17},{21,5},{4,21},{20,4},{8,20},{24,8},{9,... | collective-permute-start | bytes 3244040 | tf_op jit(solution)/shard_map/ppermute | solution.py:761
  170.4 19.2 %collective-permute-start = (s32[16]{0:T(128)S(1)}, s32[16]{0:T(128)S(1)}, u32[]{:S(2)}, u32[]{:S(2)}) collective-permute-start(s32[16]{0:T(128)S(1)} %pad_add_fusion), channel_id=1, source_target_pairs={{0,0},{1,16},{2,1},{3,17},{4,5},{5,21},{6,4},{7,20},{8,8},{9,24},{... | collective-permute-start | bytes 200 | tf_op jit(solution)/shard_map/ppermute | solution.py:755
  195.1 6.3 %collective-permute-start.18 = (f32[8,512]{1,0:T(8,128)S(1)}, f32[8,512]{1,0:T(8,128)S(1)}, u32[]{:S(2)}, u32[]{:S(2)}) collective-permute-start(f32[8,512]{1,0:T(8,128)S(1)} %get-tuple-element.44), channel_id=1, source_target_pairs={{0,16},{16,0},{1,17},{17,1},{5,21},{21,5},{4,20},{20,4},{8,24},{24... | collective-permute-start | bytes 49160 | tf_op jit(solution)/shard_map/ppermute | solution.py:808
  196.2 7.2 %collective-permute-start.20 = (f32[8,512]{1,0:T(8,128)S(1)}, f32[8,512]{1,0:T(8,128)S(1)}, u32[]{:S(2)}, u32[]{:S(2)}) collective-permute-start(f32[8,512]{1,0:T(8,128)S(1)} %get-tuple-element.44), channel_id=1, source_target_pairs={{16,2},{17,4},{21,6},{20,8},{24,10},{25,12},{29,14},{28,16},{31,18... | collective-permute-start | bytes 49160 | tf_op jit(solution)/shard_map/ppermute | solution.py:809
  201.4 8.6 %collective-permute-start.19 = (f32[16,512]{1,0:T(8,128)S(1)}, f32[16,512]{1,0:T(8,128)S(1)}, u32[]{:S(2)}, u32[]{:S(2)}) collective-permute-start(f32[16,512]{1,0:T(8,128)S(1)} %merge.1), channel_id=1, source_target_pairs={{0,0},{16,1},{1,2},{17,3},{5,4},{21,5},{4,6},{20,7},{8,8},{24,9},{... | collective-permute-start | bytes 98312 | tf_op jit(solution)/shard_map/ppermute | solution.py:816
  (6 other events, 64.7 us)
